TPU v7x, 32 devices: a whole 2x2x4 slice. The times are simulated.
32 devices in a mesh: groups: 2 (over x), seq: 16 (over z, y, core).
Axes of the slice: x: 2, y: 2, z: 4, core: 2. Of those that a mesh axis runs over, the one named last changes fastest.
Arguments:
- q_rows: bfloat16 [4096, 2048], P(('groups', 'seq')), parts along dimension 0, may hold values from -6 to 6
- k_rows: bfloat16 [4096, 2048], P(('groups', 'seq')), parts along dimension 0, may hold values from -6 to 6
- v_rows: bfloat16 [4096, 2048], P(('groups', 'seq')), parts along dimension 0, may hold values from -6 to 6
- block_of: int32 [4096, 1], P(('groups', 'seq')), parts along dimension 0, may hold values from 0 to 15; in each aligned block of 128 rows (0 to 127, 128 to 255, ...) at most 12 rows name the same one
- modality: int32 [4096], P(('groups', 'seq')), parts along dimension 0, may hold values from 0 to 2
- out_gain: float32 [3, 2048], replicated, may hold values from 0.1 to 1.9
Outputs:
- mixed: bfloat16 [4096, 2048], P(('groups', 'seq')), parts along dimension 0
There are 2 independent parts, one for each index of `groups`. A program takes and returns all parts, laid end to end along the dimension named above; an argument that names none is the same for every part. Nothing has to cross between parts.
Inputs may be any that keep to these rules, and one draw needn't show every extreme that they name: `block_of`: among the rows of one device no block is named more than 12 times, and some block is named exactly 12 times by the rows of some device.
All inputs are finite; a program needn't handle non-finite values.
Results may differ from a plain program's by a relative error of at most 0.0057.
Values may be sent and summed in bfloat16 or wider, within the bound.
No kernel may reach another device: no remote copies, remote signals or barrier semaphores. Data moves between devices by JAX's collectives and lax.ppermute only.
A program may use at most 192 MiB of HBM per device.

v0:
```python
import math

import jax
import jax.numpy as jnp
from jax import lax
from jax.sharding import PartitionSpec as P

HEADS = 16
HEAD_DIM = 128


def entering(part, axis, combine, identity):
    place = lax.axis_index(axis)
    gathered = lax.all_gather(part, axis)
    state = jnp.zeros_like(part) + jnp.asarray(identity, part.dtype)

    def one(lap, state):
        return combine(state, lax.dynamic_index_in_dim(gathered, lap, 0, False))

    return lax.fori_loop(0, place, one, state)


def block_state(key_rows, value_rows):
    return jnp.einsum("shd,she->hde", key_rows, value_rows, preferred_element_type=jnp.float32)


def add_states(earlier, later):
    return earlier + later


def attend(queries, row_order, key_rows, value_rows, carried):
    row_count = queries.shape[0]
    head_count = queries.shape[1]
    slot_count = key_rows.shape[0]
    group_size = math.gcd(head_count, 4)
    carried_part = jnp.einsum("rhd,hde->rhe", queries, carried, preferred_element_type=jnp.float32)
    causal = row_order[:, None] >= jnp.arange(slot_count, dtype=jnp.int32)[None, :]

    def one_group(group_id):
        query_group = lax.dynamic_slice_in_dim(queries, group_id * group_size, group_size, 1)
        key_group = lax.dynamic_slice_in_dim(key_rows, group_id * group_size, group_size, 1)
        value_group = lax.dynamic_slice_in_dim(value_rows, group_id * group_size, group_size, 1)
        scores = jnp.einsum(
            "rhd,shd->hrs", query_group, key_group, preferred_element_type=jnp.float32
        )
        weights = jnp.where(causal[None], scores, 0.0).astype(jnp.bfloat16)
        return jnp.einsum("hrs,she->rhe", weights, value_group, preferred_element_type=jnp.float32)

    pieces = lax.map(one_group, jnp.arange(head_count // group_size, dtype=jnp.int32))
    local_part = jnp.moveaxis(pieces, 0, 1).reshape(row_count, head_count, queries.shape[2])
    combined = carried_part + local_part
    scale = lax.rsqrt(jnp.mean(combined * combined, axis=-1, keepdims=True) + 1e-06)
    return (combined * scale).astype(jnp.bfloat16)


def on_device(q_rows, k_rows, v_rows, block_of, modality, out_gain):
    tok_count = q_rows.shape[0]
    row_width = q_rows.shape[1]
    peer_count = lax.axis_size("seq")
    capacity = max(2, 3 * tok_count // (2 * peer_count))
    slot_count = peer_count * capacity
    head_count = HEADS
    head_size = HEAD_DIM
    target = block_of[:, 0]
    member = (target[:, None] == jnp.arange(peer_count, dtype=jnp.int32)[None, :]).astype(jnp.int32)
    slot_rank = jnp.sum((jnp.cumsum(member, axis=0) - 1) * member, axis=1)
    slot_index = target * capacity + slot_rank

    def packed(row_block):
        buffer = jnp.zeros((slot_count, row_width), row_block.dtype).at[slot_index].set(row_block)
        return buffer.reshape(peer_count, capacity, row_width)

    q_send = packed(q_rows)
    k_send = packed(k_rows)
    v_send = packed(v_rows)
    q_recv, k_recv, v_recv = (
        lax.all_to_all(q_send, "seq", split_axis=0, concat_axis=0, tiled=True),
        lax.all_to_all(k_send, "seq", split_axis=0, concat_axis=0, tiled=True),
        lax.all_to_all(v_send, "seq", split_axis=0, concat_axis=0, tiled=True),
    )
    key_rows = k_recv.reshape(slot_count, head_count, head_size)
    value_rows = v_recv.reshape(slot_count, head_count, head_size)
    block_sum = block_state(key_rows, value_rows)
    prefix = entering(block_sum, "seq", add_states, jnp.zeros_like(block_sum))
    carried = prefix.astype(jnp.bfloat16)
    queries = q_recv.reshape(slot_count, head_count, head_size)
    normed = attend(queries, jnp.arange(slot_count, dtype=jnp.int32), key_rows, value_rows, carried)
    returned = lax.all_to_all(
        normed.reshape(peer_count, capacity, row_width),
        "seq",
        split_axis=0,
        concat_axis=0,
        tiled=True,
    )
    own_rows = returned.reshape(slot_count, row_width)[slot_index]
    chosen = modality[:, None]
    gains = jnp.where(
        chosen == 0,
        out_gain[0][None, :],
        jnp.where(chosen == 1, out_gain[1][None, :], out_gain[2][None, :]),
    )
    return (own_rows.astype(jnp.float32) * gains).astype(jnp.bfloat16)


def solution(mesh):
    placed = (
        P(("groups", "seq"), None),
        P(("groups", "seq"), None),
        P(("groups", "seq"), None),
        P(("groups", "seq"), None),
        P(("groups", "seq")),
        P(),
    )
    return jax.shard_map(
        on_device, mesh=mesh, in_specs=placed, out_specs=P(("groups", "seq"), None), check_vma=False
    )
```

profile of v0, /device:TPU:9, one launch (start us, length us, event | category | flops | bytes accessed | tf_op | source)
XLA Modules:
  0.0 287.0 jit_solution(9544114790081609818)
XLA Ops:
  8.9 2.1 scatter_custom_fusion
  12.3 6.6 %all-to-all-start = ((bf16[16,12,2048]{2,1,0:T(8,128)(2,1)}), bf16[16,12,2048]{2,1,0:T(8,128)(2,1)S(1)}, u32[]{:S(2)}, u32[]{:S(2)}) async-start(bf16[16,12,2048]{2,1,0:T(8,128)(2,1)} %reshape.43), calls=%async_computation | async-start | bytes 2097152 | tf_op jit(solution)/shard_map/all_to_all | solution.py:78
  18.8 2.1 scatter_custom_fusion.1
  22.1 21.7 %all-to-all-done = bf16[16,12,2048]{2,1,0:T(8,128)(2,1)S(1)} async-done(((bf16[16,12,2048]{2,1,0:T(8,128)(2,1)}), bf16[16,12,2048]{2,1,0:T(8,128)(2,1)S(1)}, u32[]{:S(2)}, u32[]{:S(2)}) %all-to-all-start) | async-done | bytes 786464 | tf_op jit(solution)/shard_map/all_to_all | solution.py:78
  43.8 4.8 %all-to-all-start.1 = ((bf16[16,12,2048]{2,1,0:T(8,128)(2,1)}), bf16[16,12,2048]{2,1,0:T(8,128)(2,1)S(1)}, u32[]{:S(2)}, u32[]{:S(2)}) async-start(bf16[16,12,2048]{2,1,0:T(8,128)(2,1)} %reshape.45), calls=%async_computation.1 | async-start | bytes 2097152 | tf_op jit(solution)/shard_map/all_to_all | solution.py:79
  49.1 24.3 %all-to-all-done.1 = bf16[16,12,2048]{2,1,0:T(8,128)(2,1)S(1)} async-done(((bf16[16,12,2048]{2,1,0:T(8,128)(2,1)}), bf16[16,12,2048]{2,1,0:T(8,128)(2,1)S(1)}, u32[]{:S(2)}, u32[]{:S(2)}) %all-to-all-start.1) | async-done | bytes 786464 | tf_op jit(solution)/shard_map/all_to_all | solution.py:79
  75.5 2.1 scatter_custom_fusion.2
  78.8 4.8 %all-to-all-start.2 = ((bf16[16,12,2048]{2,1,0:T(8,128)(2,1)}), bf16[16,12,2048]{2,1,0:T(8,128)(2,1)S(1)}, u32[]{:S(2)}, u32[]{:S(2)}) async-start(bf16[16,12,2048]{2,1,0:T(8,128)(2,1)} %reshape.47), calls=%async_computation.2 | async-start | bytes 2097152 | tf_op jit(solution)/shard_map/all_to_all | solution.py:77
  84.9 47.1 %all-to-all-done.2 = bf16[16,12,2048]{2,1,0:T(8,128)(2,1)S(1)} async-done(((bf16[16,12,2048]{2,1,0:T(8,128)(2,1)}), bf16[16,12,2048]{2,1,0:T(8,128)(2,1)S(1)}, u32[]{:S(2)}, u32[]{:S(2)}) %all-to-all-start.2) | async-done | bytes 786464 | tf_op jit(solution)/shard_map/all_to_all | solution.py:77
  132.7 13.9 %while.22 = (s32[]{:T(128)}, f32[4,192,4,128]{3,1,2,0:T(8,128)}, s32[4]{0:T(128)S(1)}, bf16[192,16,128]{2,0,1:T(8,128)(2,1)}, bf16[192,16,128]{2,0,1:T(8,128)(2,...) while((s32[]{:T(128)}, f32[4,192,4,128]{3,1,2,0:T(8,128)}, ...), condition=%wide.region_8.9_spmd.clone, body=%wide.region_7.8_spmd.clone.sunk | while | flops 75829256 | bytes 1071263 | solution.py:49
  134.1 2.1 fusion.37
  137.6 2.1 fusion.37
  141.1 2.1 fusion.37
  144.5 2.1 fusion.37
  146.6 75.3 %all-gather.3.cloned.1.call-done = f32[256,128,128]{2,1,0:T(8,128)} async-done(((f32[16,128,128]{2,1,0:T(8,128)}), f32[256,128,128]{2,1,0:T(8,128)}) %all-gather.3.cloned.1.call-update) | async-done | bytes 16777232 | tf_op jit(solution)/shard_map/all_gather | solution.py:14
  222.0 7.7 %while.21 = (s32[]{:T(128)}, f32[16,128,128]{2,1,0:T(8,128)S(1)}, s32[]{:T(128)}, f32[16,16,128,128]{3,2,1,0:T(8,128)}, s32[]{:T(128)}, /*index=5*/s32[]{:T(128)}, s32[]{:T(128)}) while((s32[]{:T(128)}, f32[16,128,128]{2,1,0:T(8,128)S(1)}, s32[]{:T(128)}, f32[16,16,128,128]{3,2,1,0:T(8,128)}, s32[]{:T(128)}, /*index=5*/s32[]{:T(128)}, ...), condition=%wide.region_5.6_spmd, body=%wide.region_4.5_spmd.sunk | while | flops 262149 | bytes 3145843 | solution.py:20
  222.0 1.6 bitcast_add_fusion.4
  223.7 1.5 bitcast_add_fusion.4
  225.2 1.5 bitcast_add_fusion.4
  226.7 1.5 bitcast_add_fusion.4
  228.2 1.5 bitcast_add_fusion.4
  231.8 1.5 reshape.50
  233.3 19.8 %all-to-all-start.3 = ((bf16[16,12,2048]{2,1,0:T(8,128)(2,1)}), bf16[16,12,2048]{2,1,0:T(8,128)(2,1)S(1)}, u32[]{:S(2)}, u32[]{:S(2)}) async-start(bf16[16,12,2048]{2,1,0:T(8,128)(2,1)} %reshape.50), calls=%async_computation.3 | async-start | bytes 2097152 | tf_op jit(solution)/shard_map/all_to_all | solution.py:88
  253.1 24.9 %all-to-all-done.3 = bf16[16,12,2048]{2,1,0:T(8,128)(2,1)S(1)} async-done(((bf16[16,12,2048]{2,1,0:T(8,128)(2,1)}), bf16[16,12,2048]{2,1,0:T(8,128)(2,1)S(1)}, u32[]{:S(2)}, u32[]{:S(2)}) %all-to-all-start.3) | async-done | bytes 786464 | tf_op jit(solution)/shard_map/all_to_all | solution.py:88
  (44 shorter events, 17.6 us)
Async XLA Ops:
  12.3 31.5 %all-to-all-start = ((bf16[16,12,2048]{2,1,0:T(8,128)(2,1)}), bf16[16,12,2048]{2,1,0:T(8,128)(2,1)S(1)}, u32[]{:S(2)}, u32[]{:S(2)}) async-start(bf16[16,12,2048]{2,1,0:T(8,128)(2,1)} %reshape.43), calls=%async_computation | async-start | bytes 2097152 | tf_op jit(solution)/shard_map/all_to_all | solution.py:78
  43.8 29.7 %all-to-all-start.1 = ((bf16[16,12,2048]{2,1,0:T(8,128)(2,1)}), bf16[16,12,2048]{2,1,0:T(8,128)(2,1)S(1)}, u32[]{:S(2)}, u32[]{:S(2)}) async-start(bf16[16,12,2048]{2,1,0:T(8,128)(2,1)} %reshape.45), calls=%async_computation.1 | async-start | bytes 2097152 | tf_op jit(solution)/shard_map/all_to_all | solution.py:79
  48.5 173.4 %all-gather.3.cloned.1.call-start = ((), (), s32[]{:S(2)}) async-start(), calls=%async_computation.4 | async-start | bytes 17825792 | tf_op jit(solution)/shard_map/all_gather | solution.py:14
  78.8 53.1 %all-to-all-start.2 = ((bf16[16,12,2048]{2,1,0:T(8,128)(2,1)}), bf16[16,12,2048]{2,1,0:T(8,128)(2,1)S(1)}, u32[]{:S(2)}, u32[]{:S(2)}) async-start(bf16[16,12,2048]{2,1,0:T(8,128)(2,1)} %reshape.47), calls=%async_computation.2 | async-start | bytes 2097152 | tf_op jit(solution)/shard_map/all_to_all | solution.py:77
  222.0 7.7 %copy-start = (f32[4,192,4,128]{3,1,2,0:T(8,128)S(1)}, f32[4,192,4,128]{3,1,2,0:T(8,128)}, u32[]{:S(2)}) copy-start(f32[4,192,4,128]{3,1,2,0:T(8,128)} %get-tuple-element.66) | copy-start | bytes 4718596
  231.8 21.3 %copy-start.2 = (s32[128]{0:T(128)S(1)}, s32[128]{0:T(128)}, u32[]{:S(2)}) copy-start(s32[128]{0:T(128)} %param.14) | copy-start | bytes 1540
  231.8 21.3 %copy-start.1 = (f32[3,2048]{1,0:T(4,128)S(1)}, f32[3,2048]{1,0:T(4,128)}, u32[]{:S(2)}) copy-start(f32[3,2048]{1,0:T(4,128)} %param.15) | copy-start | bytes 73732
  233.3 44.7 %all-to-all-start.3 = ((bf16[16,12,2048]{2,1,0:T(8,128)(2,1)}), bf16[16,12,2048]{2,1,0:T(8,128)(2,1)S(1)}, u32[]{:S(2)}, u32[]{:S(2)}) async-start(bf16[16,12,2048]{2,1,0:T(8,128)(2,1)} %reshape.50), calls=%async_computation.3 | async-start | bytes 2097152 | tf_op jit(solution)/shard_map/all_to_all | solution.py:88
Sparse Core Ops, SparseCore 0:
  75.6 146.2 all-gather.2
where the time goes:
time: 288 us; the launch traced here: 287 us
  waiting for transfers between devices  193 us (67%)
  starting transfers between devices  35.9 us (12%)
  local copies, waits for them, and re-layouts  18.9 us (7%)
  between operations  13.6 us (5%)
  other arithmetic  12.2 us (4%)
  matrix products  10.2 us (4%)
  loops' own time  2.98 us (1%)
    all_gather x1, waiting for transfers between devices, entering(): gathered = lax.all_gather(part, axis)  75.3 us
    all_to_all x1, waiting for transfers between devices, on_device(): lax.all_to_all(q_send, 'seq', split_axis=0, concat_axis=0, tiled=True)  47.1 us
    all_to_all x1, waiting for transfers between devices, on_device(): lax.all_to_all(normed.reshape(peer_count, capacity, row_width), 'seq', sp...  24.9 us
    all_to_all x1, waiting for transfers between devices, on_device(): lax.all_to_all(v_send, 'seq', split_axis=0, concat_axis=0, tiled=True)  24.3 us
    all_to_all x1, waiting for transfers between devices, on_device(): lax.all_to_all(k_send, 'seq', split_axis=0, concat_axis=0, tiled=True)  21.7 us
    all_to_all x1, starting transfers between devices, on_device(): lax.all_to_all(normed.reshape(peer_count, capacity, row_width), 'seq', sp...  19.8 us
    dot_general x4, matrix products, one_group(): jnp.einsum('hrs,she->rhe', weights, value_group, preferred_element_type=j...  8.36 us
    add x5, other arithmetic, add_states(): return earlier + later  7.55 us
  transfers between devices with their start and end apart: 5, of which 5 were waited for; matrix products, arithmetic and copies ran while one was open for 7% of the time, Pallas kernels for 0%

commit v1 on v0

--- a/solution.py
+++ b/solution.py
@@ -3,6 +3,8 @@
 import jax
 import jax.numpy as jnp
 from jax import lax
+from jax.experimental import pallas as pl
+from jax.experimental.pallas import tpu as pltpu
 from jax.sharding import PartitionSpec as P
 
 HEADS = 16
@@ -53,7 +55,7 @@
     return (combined * scale).astype(jnp.bfloat16)
 
 
-def on_device(q_rows, k_rows, v_rows, block_of, modality, out_gain):
+def by_blocks(q_rows, k_rows, v_rows, block_of, modality, out_gain):
     tok_count = q_rows.shape[0]
     row_width = q_rows.shape[1]
     peer_count = lax.axis_size("seq")
@@ -102,6 +104,101 @@
     return (own_rows.astype(jnp.float32) * gains).astype(jnp.bfloat16)
 
 
+def pack_kernel(q_ref, k_ref, v_ref, block_ref, out_ref):
+    rows = q_ref.shape[0]
+    size = out_ref.shape[2]
+    tail = out_ref.shape[1] - 3 * rows
+    marks = jnp.broadcast_to(block_ref[...].astype(jnp.float32), (tail, rows)).astype(out_ref.dtype)
+    for head in range(out_ref.shape[0]):
+        columns = pl.ds(head * size, size)
+        out_ref[head, 0:rows, :] = q_ref[:, columns]
+        out_ref[head, rows : 2 * rows, :] = k_ref[:, columns]
+        out_ref[head, 2 * rows : 3 * rows, :] = v_ref[:, columns]
+        out_ref[head, 3 * rows :, :] = marks
+
+
+def head_kernel(in_ref, out_ref):
+    peers, rows, size = out_ref.shape
+    total = peers * rows
+    marks = in_ref[:, 3 * rows, :].astype(jnp.float32)
+    row_id = lax.broadcasted_iota(jnp.int32, (peers, rows), 0) * rows
+    row_id = row_id + lax.broadcasted_iota(jnp.int32, (peers, rows), 1)
+    key_row = marks * total + row_id.astype(jnp.float32)
+    key_column = key_row.T
+    step = math.gcd(peers, 4)
+    for peer in range(peers):
+        queries = in_ref[peer, 0:rows, :]
+        place = key_column[:, peer : peer + 1]
+        combined = jnp.zeros((rows, size), jnp.float32)
+        for first in range(0, peers, step):
+            keys = in_ref[first : first + step, rows : 2 * rows, :].reshape(step * rows, size)
+            values = in_ref[first : first + step, 2 * rows : 3 * rows, :].reshape(step * rows, size)
+            other = jnp.concatenate([key_row[i : i + 1, :] for i in range(first, first + step)], axis=1)
+            scores = lax.dot_general(
+                queries, keys, (((1,), (1,)), ((), ())), preferred_element_type=jnp.float32
+            )
+            weights = jnp.where(place >= other, scores, 0.0).astype(jnp.bfloat16)
+            combined = combined + jnp.dot(weights, values, preferred_element_type=jnp.float32)
+        scale = lax.rsqrt(jnp.mean(combined * combined, axis=-1, keepdims=True) + 1e-06)
+        out_ref[peer] = (combined * scale).astype(out_ref.dtype)
+
+
+def unpack_kernel(in_ref, mode_ref, gain_ref, out_ref):
+    heads, rows, size = in_ref.shape
+    modes = jnp.broadcast_to(mode_ref[...].astype(jnp.float32), (8, rows)).T[:, 0:1]
+    for head in range(heads):
+        columns = pl.ds(head * size, size)
+        gains = jnp.where(
+            modes == 0.0,
+            gain_ref[0:1, columns],
+            jnp.where(modes == 1.0, gain_ref[1:2, columns], gain_ref[2:3, columns]),
+        )
+        out_ref[:, columns] = (in_ref[head].astype(jnp.float32) * gains).astype(out_ref.dtype)
+
+
+def by_heads(q_rows, k_rows, v_rows, block_of, modality, out_gain):
+    rows = q_rows.shape[0]
+    peers = lax.axis_size("seq")
+    size = HEAD_DIM
+    tail = 16
+    tall = 3 * rows + tail
+    step = math.gcd(peers, 4)
+    packed = pl.pallas_call(
+        pack_kernel,
+        grid=(peers // step,),
+        in_specs=[pl.BlockSpec((rows, step * size), lambda i: (0, i))] * 3
+        + [pl.BlockSpec((1, rows), lambda i: (0, 0))],
+        out_specs=pl.BlockSpec((step, tall, size), lambda i: (i, 0, 0)),
+        out_shape=jax.ShapeDtypeStruct((peers, tall, size), q_rows.dtype),
+    )(q_rows, k_rows, v_rows, block_of.reshape(1, rows))
+    arrived = lax.all_to_all(packed, "seq", split_axis=0, concat_axis=0, tiled=True)
+    normed = pl.pallas_call(
+        head_kernel,
+        in_specs=[pl.BlockSpec(memory_space=pltpu.VMEM)],
+        out_specs=pl.BlockSpec(memory_space=pltpu.VMEM),
+        out_shape=jax.ShapeDtypeStruct((peers, rows, size), q_rows.dtype),
+    )(arrived)
+    returned = lax.all_to_all(normed, "seq", split_axis=0, concat_axis=0, tiled=True)
+    return pl.pallas_call(
+        unpack_kernel,
+        grid=(peers // step,),
+        in_specs=[
+            pl.BlockSpec((step, rows, size), lambda i: (i, 0, 0)),
+            pl.BlockSpec((1, rows), lambda i: (0, 0)),
+            pl.BlockSpec((out_gain.shape[0], step * size), lambda i: (0, i)),
+        ],
+        out_specs=pl.BlockSpec((rows, step * size), lambda i: (0, i)),
+        out_shape=jax.ShapeDtypeStruct(q_rows.shape, q_rows.dtype),
+    )(returned, modality.reshape(1, rows), out_gain)
+
+
+def on_device(q_rows, k_rows, v_rows, block_of, modality, out_gain):
+    rows = q_rows.shape[0]
+    fits = lax.axis_size("seq") == HEADS and rows == HEAD_DIM
+    plan = by_heads if fits else by_blocks
+    return plan(q_rows, k_rows, v_rows, block_of, modality, out_gain)
+
+
 def solution(mesh):
     placed = (
         P(("groups", "seq"), None),

time: 288 us -> 85.2 us (0.30)
  waiting for transfers between devices: 193 us -> 0 us
  blocking collectives: 0 us -> 64.7 us
  starting transfers between devices: 35.9 us -> 0 us
  Pallas kernels: 0 us -> 19.1 us
  local copies, waits for them, and re-layouts: 18.9 us -> 0 us
  between operations: 13.6 us -> 0.01 us
  other arithmetic: 12.2 us -> 0 us
  matrix products: 10.2 us -> 0 us
  loops' own time: 2.98 us -> 0 us
    all_to_all x4 -> x0, waiting for transfers between devices: 118 us -> none  [the longest x1 47.1 us: on_device(): lax.all_to_all(q_send, 'seq', split_axis=0, concat_axis=0, tiled=True)]
    all_gather x1 -> x0, waiting for transfers between devices: 75.3 us -> none  [entering(): gathered = lax.all_gather(part, axis)]
    all_to_all x0 -> x2, blocking collectives: none -> 64.7 us  [the longest x1 45.1 us: by_heads(): lax.all_to_all(packed, 'seq', split_axis=0, concat_axis=0, tiled=True)]
    all_to_all x4 -> x0, starting transfers between devices: 35.9 us -> none  [the longest x1 19.8 us: on_device(): lax.all_to_all(normed.reshape(peer_count, capacity, row_width), 'seq', sp...]
    pallas_call x0 -> x3, Pallas kernels: none -> 19.1 us  [the longest x1 11.8 us: by_heads(): pl.pallas_call(head_kernel, in_specs=[pl.BlockSpec(memory_space=pltpu.VME...]
    dot_general x6 -> x0, matrix products: 10.2 us -> none  [the longest x4 8.36 us: one_group(): jnp.einsum('hrs,she->rhe', weights, value_group, preferred_element_type=j...]
    reshape x11 -> x0, local copies, waits for them, and re-layouts: 8.32 us -> none  [the longest x3 3.51 us: packed(): return buffer.reshape(peer_count, capacity, row_width)]
    add x5 -> x0, other arithmetic: 7.55 us -> none  [add_states(): return earlier + later]
  transfers between devices with their start and end apart: 5 -> 0, of which waited for: 5 -> 0; matrix products, arithmetic and copies ran while one was open for 7% -> 0% of each run, Pallas kernels for 0% -> 0%
where the time goes in v1:
time: 85.2 us; the launch traced here: 83.8 us
  blocking collectives  64.7 us (76%)
  Pallas kernels  19.1 us (22%)
    all_to_all x1, blocking collectives, by_heads(): lax.all_to_all(packed, 'seq', split_axis=0, concat_axis=0, tiled=True)  45.1 us
    all_to_all x1, blocking collectives, by_heads(): lax.all_to_all(normed, 'seq', split_axis=0, concat_axis=0, tiled=True)  19.6 us
    pallas_call x1, Pallas kernels, by_heads(): pl.pallas_call(head_kernel, in_specs=[pl.BlockSpec(memory_space=pltpu.VME...  11.8 us
    pallas_call x1, Pallas kernels, by_heads(): pl.pallas_call(pack_kernel, grid=(peers // step,), in_specs=[pl.BlockSpec...  3.73 us
    pallas_call x1, Pallas kernels, by_heads(): pl.pallas_call(unpack_kernel, grid=(peers // step,), in_specs=[pl.BlockSp...  3.54 us

profile of v1, /device:TPU:9, one launch (start us, length us, event | category | flops | bytes accessed | tf_op | source)
XLA Modules:
  0.0 83.8 jit_solution(2455934644638863904)
XLA Ops:
  0.0 3.7 %shard_map.64 = bf16[16,400,128]{2,1,0:T(8,128)(2,1)} custom-call(bf16[128,2048]{1,0:T(8,128)(2,1)} %q_ref.1, bf16[128,2048]{1,0:T(8,128)(2,1)} %k_ref.1, bf16[128,2048]{1,0:T(8,128)(2,1)} %v_ref.1, s32[1,128]{1,0:T(1,128)} %bitcast.3), custom_call_target="tpu_custom_call" | custom-call | tf_op jit(solution)/shard_map/pallas_call | solution.py:166
  3.7 45.1 %all_to_all.10.in_ref = bf16[16,400,128]{2,1,0:T(8,128)(2,1)} all-to-all(bf16[16,400,128]{2,1,0:T(8,128)(2,1)} %shard_map.64), channel_id=1, replica_groups=mesh['groups'=2,'seq'=16] {'seq'}, dimensions={0} | all-to-all | bytes 3276800 | tf_op jit(solution)/shard_map/all_to_all | solution.py:174
  48.8 11.8 %shard_map.65 = bf16[16,128,128]{2,1,0:T(8,128)(2,1)} custom-call(bf16[16,400,128]{2,1,0:T(8,128)(2,1)} %all_to_all.10.in_ref), custom_call_target="tpu_custom_call" | custom-call | tf_op jit(solution)/shard_map/pallas_call | solution.py:175
  60.6 19.6 %all_to_all.11.in_ref = bf16[16,128,128]{2,1,0:T(8,128)(2,1)} all-to-all(bf16[16,128,128]{2,1,0:T(8,128)(2,1)} %shard_map.65), channel_id=1, replica_groups=mesh['groups'=2,'seq'=16] {'seq'}, dimensions={0} | all-to-all | bytes 1048576 | tf_op jit(solution)/shard_map/all_to_all | solution.py:181
  80.2 3.5 %shard_map.66 = bf16[128,2048]{1,0:T(8,128)(2,1)} custom-call(bf16[16,128,128]{2,1,0:T(8,128)(2,1)} %all_to_all.11.in_ref, s32[1,128]{1,0:T(1,128)} %bitcast.2, f32[3,2048]{1,0:T(4,128)} %gain_ref.1), custom_call_target="tpu_custom_call" | custom-call | tf_op jit(solution)/shard_map/pallas_call | solution.py:182

commit v2 on v0

--- a/solution.py
+++ b/solution.py
@@ -1,12 +1,20 @@
+import functools
 import math
 
 import jax
 import jax.numpy as jnp
 from jax import lax
+from jax.experimental import pallas as pl
+from jax.experimental.pallas import tpu as pltpu
 from jax.sharding import PartitionSpec as P
 
 HEADS = 16
 HEAD_DIM = 128
+TAIL = 16
+LATE = 2
+TILE = 2
+VMEM = pl.BlockSpec(memory_space=pltpu.VMEM)
+SMEM = pl.BlockSpec(memory_space=pltpu.SMEM)
 
 
 def entering(part, axis, combine, identity):
@@ -53,7 +61,7 @@
     return (combined * scale).astype(jnp.bfloat16)
 
 
-def on_device(q_rows, k_rows, v_rows, block_of, modality, out_gain):
+def by_blocks(q_rows, k_rows, v_rows, block_of, modality, out_gain):
     tok_count = q_rows.shape[0]
     row_width = q_rows.shape[1]
     peer_count = lax.axis_size("seq")
@@ -102,6 +110,199 @@
     return (own_rows.astype(jnp.float32) * gains).astype(jnp.bfloat16)
 
 
+def pack_kernel(to_ref, q_ref, k_ref, v_ref, block_ref, *out_refs):
+    rows = q_ref.shape[0]
+    size = out_refs[0].shape[-1]
+    marks = jnp.broadcast_to(block_ref[...].astype(jnp.float32), (TAIL, rows)).astype(q_ref.dtype)
+    views = [out for out in out_refs]
+    if len(out_refs[0].shape) == 3:
+        views = [out_refs[0].at[i] for i in range(out_refs[0].shape[0])]
+    for i, view in enumerate(views):
+        columns = pl.ds(pl.multiple_of(to_ref[i] * size, size), size)
+        view[0:rows, :] = q_ref[:, columns]
+        view[rows : 2 * rows, :] = k_ref[:, columns]
+        view[2 * rows : 3 * rows, :] = v_ref[:, columns]
+        view[3 * rows :, :] = marks
+
+
+def pack(to, whole, q_rows, k_rows, v_rows, marks):
+    count = to.shape[0]
+    rows = q_rows.shape[0]
+    one = (3 * rows + TAIL, HEAD_DIM)
+    shapes = [(count,) + one] if whole else [one] * count
+    out = pl.pallas_call(
+        pack_kernel,
+        in_specs=[SMEM] + [VMEM] * 4,
+        out_specs=[VMEM] * len(shapes),
+        out_shape=[jax.ShapeDtypeStruct(shape, q_rows.dtype) for shape in shapes],
+        compiler_params=pltpu.CompilerParams(vmem_limit_bytes=8 << 20),
+        cost_estimate=pl.CostEstimate(flops=1 << 20, bytes_accessed=count << 18, transcendentals=0),
+    )(to, q_rows, k_rows, v_rows, marks)
+    return out[0] if whole else out
+
+
+def load_chunks(first, chunks, rows, from_ref, q_ref, k_ref, v_ref, key_ref, column_ref):
+    total = rows * from_ref.shape[0]
+    size = q_ref.shape[1]
+    for i, chunk in enumerate(chunks):
+        at = (first + i) * rows
+        q_ref[at : at + rows, :] = chunk[0:rows, :]
+        k_ref[at : at + rows, :] = chunk[rows : 2 * rows, :]
+        v_ref[at : at + rows, :] = chunk[2 * rows : 3 * rows, :]
+        marks = chunk[3 * rows : 3 * rows + TAIL, :].astype(jnp.float32)[0:1, :]
+        row_id = lax.broadcasted_iota(jnp.int32, (1, rows), 1) + from_ref[first + i] * rows
+        key_ref[first + i : first + i + 1, :] = marks * total + row_id.astype(jnp.float32)
+    columns = key_ref[...].T
+    for i in range(first, first + len(chunks)):
+        column_ref[i * rows : (i + 1) * rows, :] = jnp.broadcast_to(columns[:, i : i + 1], (rows, size))
+
+
+def attend_tiles(queries, chunks, rows, start, q_ref, k_ref, v_ref, key_ref, column_ref):
+    low, high = queries
+    total = start
+    query = q_ref[low:high, :]
+    for first in range(chunks[0], chunks[1], TILE):
+        last = min(first + TILE, chunks[1])
+        keys = k_ref[first * rows : last * rows, :]
+        values = v_ref[first * rows : last * rows, :]
+        scores = lax.dot_general(
+            query, keys, (((1,), (1,)), ((), ())), preferred_element_type=jnp.float32
+        )
+        column = column_ref[low:high, 0:rows]
+        weights = jnp.concatenate(
+            [
+                jnp.where(
+                    column >= key_ref[i : i + 1, :],
+                    scores[:, (i - first) * rows : (i - first + 1) * rows],
+                    0.0,
+                ).astype(jnp.bfloat16)
+                for i in range(first, last)
+            ],
+            axis=1,
+        )
+        part = jnp.dot(weights, values, preferred_element_type=jnp.float32)
+        total = part if total is None else total + part
+    return total
+
+
+def early_kernel(far, from_ref, near_ref, *refs):
+    far_refs, (sum_ref, *scratch) = refs[:far], refs[far:]
+    near = near_ref.shape[0]
+    rows = sum_ref.shape[0] // (near + far)
+    chunks = [near_ref.at[i] for i in range(near)] + list(far_refs)
+    load_chunks(0, chunks, rows, from_ref, *scratch)
+    sum_ref[...] = attend_tiles((0, (near + far) * rows), (0, near + far), rows, None, *scratch)
+
+
+def late_kernel(far, from_ref, sum_ref, near_ref, *refs):
+    far_refs, (out_ref, *scratch) = refs[:far], refs[far:]
+    near = near_ref.shape[0]
+    peers, rows, _ = out_ref.shape
+    chunks = [near_ref.at[i] for i in range(near)] + list(far_refs)
+    load_chunks(0, chunks, rows, from_ref, *scratch)
+    early = peers - LATE
+    for low, high, start, keys in (
+        (0, early, sum_ref[...], (early, peers)),
+        (early, peers, None, (0, peers)),
+    ):
+        combined = attend_tiles((low * rows, high * rows), keys, rows, start, *scratch)
+        scale = lax.rsqrt(jnp.mean(combined * combined, axis=-1, keepdims=True) + 1e-06)
+        normed = (combined * scale).astype(out_ref.dtype)
+        for i in range(low, high):
+            out_ref[from_ref[i]] = normed[(i - low) * rows : (i - low + 1) * rows, :]
+
+
+def attention_scratch(peers, rows):
+    return [pltpu.VMEM((peers * rows, HEAD_DIM), jnp.bfloat16)] * 3 + [
+        pltpu.VMEM((peers, rows), jnp.float32),
+        pltpu.VMEM((peers * rows, HEAD_DIM), jnp.float32),
+    ]
+
+
+def unpack_kernel(in_ref, mode_ref, gain_ref, out_ref):
+    heads, rows, size = in_ref.shape
+    modes = jnp.broadcast_to(mode_ref[...].astype(jnp.float32), (8, rows)).T[:, 0:1]
+    modes = jnp.broadcast_to(modes, (rows, size))
+    for head in range(heads):
+        columns = pl.ds(head * size, size)
+        gains = jnp.where(
+            modes == 0.0,
+            gain_ref[0:1, columns],
+            jnp.where(modes == 1.0, gain_ref[1:2, columns], gain_ref[2:3, columns]),
+        )
+        out_ref[:, columns] = (in_ref[head].astype(jnp.float32) * gains).astype(out_ref.dtype)
+
+
+def by_heads(q_rows, k_rows, v_rows, block_of, modality, out_gain):
+    rows = q_rows.shape[0]
+    peers = lax.axis_size("seq")
+    half = peers // 2
+    me = lax.axis_index("seq")
+    base = (me // half) * half
+    marks = block_of.reshape(1, rows)
+    far_bits = list(range(half, peers))
+    sources = jnp.concatenate(
+        [base + jnp.arange(half, dtype=jnp.int32), me ^ jnp.array(far_bits, dtype=jnp.int32)]
+    ).astype(jnp.int32)
+    sent = pack(sources[half : half + 2], False, q_rows, k_rows, v_rows, marks)
+    sent = sent + pack(sources[half + 2 :], False, q_rows, k_rows, v_rows, marks)
+    near_sent = pack(sources[:half], True, q_rows, k_rows, v_rows, marks)
+    far = []
+    for bit, chunk in zip(far_bits, sent):
+        far.append(lax.ppermute(chunk, "seq", [(i, i ^ bit) for i in range(peers)]))
+    near = lax.all_to_all(
+        near_sent,
+        "seq",
+        split_axis=0,
+        concat_axis=0,
+        tiled=True,
+        axis_index_groups=[list(range(half)), list(range(half, peers))],
+    )
+    early = peers - LATE
+    limit = pltpu.CompilerParams(vmem_limit_bytes=24 << 20)
+    flops = 4 * rows * rows * HEAD_DIM
+    partial_sum = pl.pallas_call(
+        functools.partial(early_kernel, early - half),
+        in_specs=[SMEM] + [VMEM] * (1 + early - half),
+        out_specs=VMEM,
+        out_shape=jax.ShapeDtypeStruct((early * rows, HEAD_DIM), jnp.float32),
+        scratch_shapes=attention_scratch(peers, rows),
+        compiler_params=limit,
+        cost_estimate=pl.CostEstimate(
+            flops=flops * early * early, bytes_accessed=1 << 20, transcendentals=0
+        ),
+    )(sources, near, *far[: early - half])
+    normed = pl.pallas_call(
+        functools.partial(late_kernel, half),
+        in_specs=[SMEM] + [VMEM] * (2 + half),
+        out_specs=VMEM,
+        out_shape=jax.ShapeDtypeStruct((peers, rows, HEAD_DIM), q_rows.dtype),
+        scratch_shapes=attention_scratch(peers, rows),
+        compiler_params=limit,
+        cost_estimate=pl.CostEstimate(
+            flops=flops * (peers * peers - early * early), bytes_accessed=1 << 20, transcendentals=0
+        ),
+    )(sources, partial_sum, near, *far)
+    returned = lax.all_to_all(normed, "seq", split_axis=0, concat_axis=0, tiled=True)
+    return pl.pallas_call(
+        unpack_kernel,
+        in_specs=[VMEM] * 3,
+        out_specs=VMEM,
+        out_shape=jax.ShapeDtypeStruct(q_rows.shape, q_rows.dtype),
+        compiler_params=pltpu.CompilerParams(vmem_limit_bytes=8 << 20),
+    )(returned, modality.reshape(1, rows), out_gain)
+
+
+def fits_heads(peers, rows):
+    return peers == HEADS and rows == HEAD_DIM and peers >= 8 and peers & (peers - 1) == 0
+
+
+def on_device(q_rows, k_rows, v_rows, block_of, modality, out_gain):
+    fits = fits_heads(lax.axis_size("seq"), q_rows.shape[0])
+    plan = by_heads if fits else by_blocks
+    return plan(q_rows, k_rows, v_rows, block_of, modality, out_gain)
+
+
 def solution(mesh):
     placed = (
         P(("groups", "seq"), None),

time: 288 us -> 75.1 us (0.26)
  waiting for transfers between devices: 193 us -> 25.1 us
  starting transfers between devices: 35.9 us -> 13.2 us
  blocking collectives: 0 us -> 19.6 us
  local copies, waits for them, and re-layouts: 18.9 us -> 4.52 us
  between operations: 13.6 us -> 0.09 us
  other arithmetic: 12.2 us -> 0.08 us
  Pallas kernels: 0 us -> 11 us
  matrix products: 10.2 us -> 0 us
  loops' own time: 2.98 us -> 0 us
    all_to_all x4 -> x1, waiting for transfers between devices: 118 us -> 0.01 us  [by_heads(): lax.all_to_all(near_sent, 'seq', split_axis=0, concat_axis=0, tiled=True,...]
    all_gather x1 -> x0, waiting for transfers between devices: 75.3 us -> none  [entering(): gathered = lax.all_gather(part, axis)]
    all_to_all x4 -> x1, starting transfers between devices: 35.9 us -> 4.68 us  [by_heads(): lax.all_to_all(near_sent, 'seq', split_axis=0, concat_axis=0, tiled=True,...]
    ppermute x0 -> x8, waiting for transfers between devices: none -> 25.1 us  [by_heads(): far.append(lax.ppermute(chunk, 'seq', [(i, i ^ bit) for i in range(peers)]))]
    all_to_all x0 -> x1, blocking collectives: none -> 19.6 us  [by_heads(): lax.all_to_all(normed, 'seq', split_axis=0, concat_axis=0, tiled=True)]
    pallas_call x0 -> x6, Pallas kernels: none -> 11 us  [the longest x1 4.77 us: by_heads(): pl.pallas_call(functools.partial(early_kernel, early - half), in_specs=[S...]
    dot_general x6 -> x0, matrix products: 10.2 us -> none  [the longest x4 8.36 us: one_group(): jnp.einsum('hrs,she->rhe', weights, value_group, preferred_element_type=j...]
    ppermute x0 -> x8, starting transfers between devices: none -> 8.47 us  [by_heads(): far.append(lax.ppermute(chunk, 'seq', [(i, i ^ bit) for i in range(peers)]))]
  transfers between devices with their start and end apart: 5 -> 9, of which waited for: 5 -> 7; matrix products, arithmetic and copies ran while one was open for 7% -> 0% of each run, Pallas kernels for 0% -> 8%
where the time goes in v2:
time: 75.1 us; the launch traced here: 73.6 us
  waiting for transfers between devices  25.1 us (33%)
  blocking collectives  19.6 us (26%)
  starting transfers between devices  13.2 us (18%)
  Pallas kernels  11 us (15%)
  local copies, waits for them, and re-layouts  4.52 us (6%)
    ppermute x8, waiting for transfers between devices, by_heads(): far.append(lax.ppermute(chunk, 'seq', [(i, i ^ bit) for i in range(peers)]))  25.1 us
    all_to_all x1, blocking collectives, by_heads(): lax.all_to_all(normed, 'seq', split_axis=0, concat_axis=0, tiled=True)  19.6 us
    ppermute x8, starting transfers between devices, by_heads(): far.append(lax.ppermute(chunk, 'seq', [(i, i ^ bit) for i in range(peers)]))  8.47 us
    pallas_call x1, Pallas kernels, by_heads(): pl.pallas_call(functools.partial(early_kernel, early - half), in_specs=[S...  4.77 us
    all_to_all x1, starting transfers between devices, by_heads(): lax.all_to_all(near_sent, 'seq', split_axis=0, concat_axis=0, tiled=True,...  4.68 us
    unnamed x20, local copies, waits for them, and re-layouts  4.45 us
    pallas_call x3, Pallas kernels, pack(): pl.pallas_call(pack_kernel, in_specs=[SMEM] + [VMEM] * 4, out_specs=[VMEM...  2.94 us
    pallas_call x1, Pallas kernels, by_heads(): pl.pallas_call(functools.partial(late_kernel, half), in_specs=[SMEM] + [V...  2.2 us
  transfers between devices with their start and end apart: 9, of which 7 were waited for; matrix products, arithmetic and copies ran while one was open for 0% of the time, Pallas kernels for 8%

profile of v2, /device:TPU:9, one launch (start us, length us, event | category | flops | bytes accessed | tf_op | source)
XLA Modules:
  0.0 73.6 jit_solution(13967129968836920029)
XLA Ops:
  0.0 0.7 copy-done.7
  0.7 1.0 %copy-done = bf16[128,2048]{1,0:T(8,128)(2,1)S(1)} copy-done((bf16[128,2048]{1,0:T(8,128)(2,1)S(1)}, bf16[128,2048]{1,0:T(8,128)(2,1)}, u32[]{:S(2)}) %copy-start) | copy-done | bytes 524312
  1.7 1.0 %copy-done.2 = bf16[128,2048]{1,0:T(8,128)(2,1)S(1)} copy-done((bf16[128,2048]{1,0:T(8,128)(2,1)S(1)}, bf16[128,2048]{1,0:T(8,128)(2,1)}, u32[]{:S(2)}) %copy-start.2) | copy-done | bytes 524312
  2.7 1.0 %copy-done.4 = bf16[128,2048]{1,0:T(8,128)(2,1)S(1)} copy-done((bf16[128,2048]{1,0:T(8,128)(2,1)S(1)}, bf16[128,2048]{1,0:T(8,128)(2,1)}, u32[]{:S(2)}) %copy-start.4) | copy-done | bytes 524312
  3.8 1.6 %shard_map.73 = bf16[8,400,128]{2,1,0:T(8,128)(2,1)} custom-call(s32[8]{0:T(128)S(1)} %iota_add_fusion.to_ref, bf16[128,2048]{1,0:T(8,128)(2,1)S(1)} %copy-done, bf16[128,2048]{1,0:T(8,128)(2,1)S(1)} %copy-done.2, bf16[128,2048]{1,0:T(8,128)(2,1)S(1)} %copy-done.4, s32[1,128]{1,0:T(1,128)S(1)} %bitcast.3), custom_call_target="tpu_custom_call" | custom-call | flops 1048576 | bytes 2097152 | tf_op jit(solution)/shard_map/pallas_call | solution.py:133
  5.4 4.7 %all-to-all-start = ((bf16[8,400,128]{2,1,0:T(8,128)(2,1)}), bf16[8,400,128]{2,1,0:T(8,128)(2,1)S(1)}, u32[]{:S(2)}, u32[]{:S(2)}) async-start(bf16[8,400,128]{2,1,0:T(8,128)(2,1)} %shard_map.73), calls=%async_computation | async-start | bytes 1638400 | tf_op jit(solution)/shard_map/all_to_all | solution.py:253
  10.8 2.4 %collective-permute-start = (bf16[400,128]{1,0:T(8,128)(2,1)S(1)}, bf16[400,128]{1,0:T(8,128)(2,1)S(1)}, u32[]{:S(2)}, u32[]{:S(2)}) collective-permute-start(bf16[400,128]{1,0:T(8,128)(2,1)S(1)} %get-tuple-element.13), channel_id=1, source_target_pairs={{0,8},{1,9},{2,10},{3,11},{4,12},{5,13},{6,14},{7,15},{8,0},{9,1},... | collective-permute-start | bytes 307208 | tf_op jit(solution)/shard_map/ppermute | solution.py:252
  13.1 0.6 collective-permute-start.1
  13.8 0.7 shard_map.75
  14.5 3.3 %collective-permute-start.2 = (bf16[400,128]{1,0:T(8,128)(2,1)S(1)}, bf16[400,128]{1,0:T(8,128)(2,1)S(1)}, u32[]{:S(2)}, u32[]{:S(2)}) collective-permute-start(bf16[400,128]{1,0:T(8,128)(2,1)S(1)} %get-tuple-element.15), channel_id=1, source_target_pairs={{0,10},{1,11},{2,8},{3,9},{4,14},{5,15},{6,12},{7,13},{8,2},{9,3},... | collective-permute-start | bytes 307208 | tf_op jit(solution)/shard_map/ppermute | solution.py:252
  18.1 1.0 %collective-permute-start.4 = (bf16[400,128]{1,0:T(8,128)(2,1)S(1)}, bf16[400,128]{1,0:T(8,128)(2,1)S(1)}, u32[]{:S(2)}, u32[]{:S(2)}) collective-permute-start(bf16[400,128]{1,0:T(8,128)(2,1)S(1)} %get-tuple-element.17), channel_id=1, source_target_pairs={{0,12},{1,13},{2,14},{3,15},{4,8},{5,9},{6,10},{7,11},{8,4},{9,5},... | collective-permute-start | bytes 307208 | tf_op jit(solution)/shard_map/ppermute | solution.py:252
  19.1 5.3 %collective-permute-done.refs_0_ = bf16[400,128]{1,0:T(8,128)(2,1)S(1)} collective-permute-done((bf16[400,128]{1,0:T(8,128)(2,1)S(1)}, bf16[400,128]{1,0:T(8,128)(2,1)S(1)}, u32[]{:S(2)}, u32[]{:S(2)}) %collective-permute-start) | collective-permute-done | bytes 102432 | tf_op jit(solution)/shard_map/ppermute | solution.py:252
  24.5 2.9 %collective-permute-done.1.refs_1_ = bf16[400,128]{1,0:T(8,128)(2,1)S(1)} collective-permute-done((bf16[400,128]{1,0:T(8,128)(2,1)S(1)}, bf16[400,128]{1,0:T(8,128)(2,1)S(1)}, u32[]{:S(2)}, u32[]{:S(2)}) %collective-permute-start.1) | collective-permute-done | bytes 102432 | tf_op jit(solution)/shard_map/ppermute | solution.py:252
  27.5 0.8 %collective-permute-start.6 = (bf16[400,128]{1,0:T(8,128)(2,1)S(1)}, bf16[400,128]{1,0:T(8,128)(2,1)S(1)}, u32[]{:S(2)}, u32[]{:S(2)}) collective-permute-start(bf16[400,128]{1,0:T(8,128)(2,1)S(1)} %get-tuple-element.19), channel_id=1, source_target_pairs={{0,14},{1,15},{2,12},{3,13},{4,10},{5,11},{6,8},{7,9},{8,6},{9,7},... | collective-permute-start | bytes 307208 | tf_op jit(solution)/shard_map/ppermute | solution.py:252
  28.3 7.1 %collective-permute-done.2.refs_2_ = bf16[400,128]{1,0:T(8,128)(2,1)S(1)} collective-permute-done((bf16[400,128]{1,0:T(8,128)(2,1)S(1)}, bf16[400,128]{1,0:T(8,128)(2,1)S(1)}, u32[]{:S(2)}, u32[]{:S(2)}) %collective-permute-start.2) | collective-permute-done | bytes 102432 | tf_op jit(solution)/shard_map/ppermute | solution.py:252
  35.4 2.3 %collective-permute-done.3.refs_3_ = bf16[400,128]{1,0:T(8,128)(2,1)S(1)} collective-permute-done((bf16[400,128]{1,0:T(8,128)(2,1)S(1)}, bf16[400,128]{1,0:T(8,128)(2,1)S(1)}, u32[]{:S(2)}, u32[]{:S(2)}) %collective-permute-start.3) | collective-permute-done | bytes 102432 | tf_op jit(solution)/shard_map/ppermute | solution.py:252
  37.8 3.3 %collective-permute-done.4.refs_4_ = bf16[400,128]{1,0:T(8,128)(2,1)S(1)} collective-permute-done((bf16[400,128]{1,0:T(8,128)(2,1)S(1)}, bf16[400,128]{1,0:T(8,128)(2,1)S(1)}, u32[]{:S(2)}, u32[]{:S(2)}) %collective-permute-start.4) | collective-permute-done | bytes 102432 | tf_op jit(solution)/shard_map/ppermute | solution.py:252
  41.1 3.3 %collective-permute-done.5.refs_5_ = bf16[400,128]{1,0:T(8,128)(2,1)S(1)} collective-permute-done((bf16[400,128]{1,0:T(8,128)(2,1)S(1)}, bf16[400,128]{1,0:T(8,128)(2,1)S(1)}, u32[]{:S(2)}, u32[]{:S(2)}) %collective-permute-start.5) | collective-permute-done | bytes 102432 | tf_op jit(solution)/shard_map/ppermute | solution.py:252
  44.4 4.8 %shard_map.76.sum_ref = f32[1792,128]{1,0:T(8,128)S(1)} custom-call(s32[16]{0:T(128)S(1)} %pad_add_fusion.from_ref, bf16[8,400,128]{2,1,0:T(8,128)(2,1)S(1)} %all-to-all-done.near_ref, bf16[400,128]{1,0:T(8,128)(2,1)S(1)} %collective-permute-done.refs_0_, bf16[400,128]{1,0:T(8,128)(2,1)S(1)} %collective-permute-done.1.refs_1_, ...), custom_call_target="tpu_custom_call" | custom-call | flops 1644167168 | bytes 1048576 | tf_op jit(solution)/shard_map/pallas_call | solution.py:264
  49.2 0.8 %collective-permute-done.7.refs_7_ = bf16[400,128]{1,0:T(8,128)(2,1)S(1)} collective-permute-done((bf16[400,128]{1,0:T(8,128)(2,1)S(1)}, bf16[400,128]{1,0:T(8,128)(2,1)S(1)}, u32[]{:S(2)}, u32[]{:S(2)}) %collective-permute-start.7) | collective-permute-done | bytes 102432 | tf_op jit(solution)/shard_map/ppermute | solution.py:252
  50.0 2.2 %shard_map.77 = bf16[16,128,128]{2,1,0:T(8,128)(2,1)S(1)} custom-call(s32[16]{0:T(128)S(1)} %pad_add_fusion.from_ref, f32[1792,128]{1,0:T(8,128)S(1)} %shard_map.76.sum_ref, bf16[8,400,128]{2,1,0:T(8,128)(2,1)S(1)} %all-to-all-done.near_ref, bf16[400,128]{1,0:T(8,128)(2,1)S(1)} %collective-permute-done.refs_0_, ...), custom_call_target="tpu_custom_call" | custom-call | flops 503316480 | bytes 1048576 | tf_op jit(solution)/shard_map/pallas_call | solution.py:275
  52.2 19.6 %all_to_all.10.in_ref = bf16[16,128,128]{2,1,0:T(8,128)(2,1)S(1)} all-to-all(bf16[16,128,128]{2,1,0:T(8,128)(2,1)S(1)} %shard_map.77), channel_id=1, replica_groups=mesh['groups'=2,'seq'=16] {'seq'}, dimensions={0} | all-to-all | bytes 1048576 | tf_op jit(solution)/shard_map/all_to_all | solution.py:286
  71.9 0.7 copy-done.8
  72.5 1.1 %shard_map.78 = bf16[128,2048]{1,0:T(8,128)(2,1)} custom-call(bf16[16,128,128]{2,1,0:T(8,128)(2,1)S(1)} %all_to_all.10.in_ref, s32[1,128]{1,0:T(1,128)S(1)} %bitcast.6, f32[3,2048]{1,0:T(4,128)S(1)} %copy-done.6), custom_call_target="tpu_custom_call" | custom-call | tf_op jit(solution)/shard_map/pallas_call | solution.py:287
  (25 shorter events, 1.1 us)
Async XLA Ops:
  0.0 0.7 copy-start.7
  0.7 1.0 %copy-start = (bf16[128,2048]{1,0:T(8,128)(2,1)S(1)}, bf16[128,2048]{1,0:T(8,128)(2,1)}, u32[]{:S(2)}) copy-start(bf16[128,2048]{1,0:T(8,128)(2,1)} %q_ref.5) | copy-start | bytes 1572868
  1.7 1.0 %copy-start.2 = (bf16[128,2048]{1,0:T(8,128)(2,1)S(1)}, bf16[128,2048]{1,0:T(8,128)(2,1)}, u32[]{:S(2)}) copy-start(bf16[128,2048]{1,0:T(8,128)(2,1)} %k_ref.5) | copy-start | bytes 1572868
  2.7 1.0 %copy-start.4 = (bf16[128,2048]{1,0:T(8,128)(2,1)S(1)}, bf16[128,2048]{1,0:T(8,128)(2,1)}, u32[]{:S(2)}) copy-start(bf16[128,2048]{1,0:T(8,128)(2,1)} %v_ref.5) | copy-start | bytes 1572868
  5.4 4.7 %copy-start.9 = (s32[8]{0:T(128)S(1)}, s32[8]{0:T(128)}, u32[]{:S(2)}) copy-start(s32[8]{0:T(128)} %constant.23.clone) | copy-start | bytes 100
  5.4 4.7 %copy-start.1 = (bf16[128,2048]{1,0:T(8,128)(2,1)S(1)}, bf16[128,2048]{1,0:T(8,128)(2,1)}, u32[]{:S(2)}) copy-start(bf16[128,2048]{1,0:T(8,128)(2,1)} %q_ref.5) | copy-start | bytes 1572868
  5.4 4.7 %copy-start.3 = (bf16[128,2048]{1,0:T(8,128)(2,1)S(1)}, bf16[128,2048]{1,0:T(8,128)(2,1)}, u32[]{:S(2)}) copy-start(bf16[128,2048]{1,0:T(8,128)(2,1)} %k_ref.5) | copy-start | bytes 1572868
  5.4 4.7 %copy-start.5 = (bf16[128,2048]{1,0:T(8,128)(2,1)S(1)}, bf16[128,2048]{1,0:T(8,128)(2,1)}, u32[]{:S(2)}) copy-start(bf16[128,2048]{1,0:T(8,128)(2,1)} %v_ref.5) | copy-start | bytes 1572868
  5.4 38.9 %all-to-all-start = ((bf16[8,400,128]{2,1,0:T(8,128)(2,1)}), bf16[8,400,128]{2,1,0:T(8,128)(2,1)S(1)}, u32[]{:S(2)}, u32[]{:S(2)}) async-start(bf16[8,400,128]{2,1,0:T(8,128)(2,1)} %shard_map.73), calls=%async_computation | async-start | bytes 1638400 | tf_op jit(solution)/shard_map/all_to_all | solution.py:253
  10.8 13.6 %collective-permute-start = (bf16[400,128]{1,0:T(8,128)(2,1)S(1)}, bf16[400,128]{1,0:T(8,128)(2,1)S(1)}, u32[]{:S(2)}, u32[]{:S(2)}) collective-permute-start(bf16[400,128]{1,0:T(8,128)(2,1)S(1)} %get-tuple-element.13), channel_id=1, source_target_pairs={{0,8},{1,9},{2,10},{3,11},{4,12},{5,13},{6,14},{7,15},{8,0},{9,1},... | collective-permute-start | bytes 307208 | tf_op jit(solution)/shard_map/ppermute | solution.py:252
  13.1 14.3 %collective-permute-start.1 = (bf16[400,128]{1,0:T(8,128)(2,1)S(1)}, bf16[400,128]{1,0:T(8,128)(2,1)S(1)}, u32[]{:S(2)}, u32[]{:S(2)}) collective-permute-start(bf16[400,128]{1,0:T(8,128)(2,1)S(1)} %get-tuple-element.14), channel_id=1, source_target_pairs={{0,9},{1,8},{2,11},{3,10},{4,13},{5,12},{6,15},{7,14},{8,1},{9,0},... | collective-permute-start | bytes 307208 | tf_op jit(solution)/shard_map/ppermute | solution.py:252
  14.5 20.9 %collective-permute-start.2 = (bf16[400,128]{1,0:T(8,128)(2,1)S(1)}, bf16[400,128]{1,0:T(8,128)(2,1)S(1)}, u32[]{:S(2)}, u32[]{:S(2)}) collective-permute-start(bf16[400,128]{1,0:T(8,128)(2,1)S(1)} %get-tuple-element.15), channel_id=1, source_target_pairs={{0,10},{1,11},{2,8},{3,9},{4,14},{5,15},{6,12},{7,13},{8,2},{9,3},... | collective-permute-start | bytes 307208 | tf_op jit(solution)/shard_map/ppermute | solution.py:252
  17.8 20.0 %collective-permute-start.3 = (bf16[400,128]{1,0:T(8,128)(2,1)S(1)}, bf16[400,128]{1,0:T(8,128)(2,1)S(1)}, u32[]{:S(2)}, u32[]{:S(2)}) collective-permute-start(bf16[400,128]{1,0:T(8,128)(2,1)S(1)} %get-tuple-element.16), channel_id=1, source_target_pairs={{0,11},{1,10},{2,9},{3,8},{4,15},{5,14},{6,13},{7,12},{8,3},{9,2},... | collective-permute-start | bytes 307208 | tf_op jit(solution)/shard_map/ppermute | solution.py:252
  18.1 23.0 %collective-permute-start.4 = (bf16[400,128]{1,0:T(8,128)(2,1)S(1)}, bf16[400,128]{1,0:T(8,128)(2,1)S(1)}, u32[]{:S(2)}, u32[]{:S(2)}) collective-permute-start(bf16[400,128]{1,0:T(8,128)(2,1)S(1)} %get-tuple-element.17), channel_id=1, source_target_pairs={{0,12},{1,13},{2,14},{3,15},{4,8},{5,9},{6,10},{7,11},{8,4},{9,5},... | collective-permute-start | bytes 307208 | tf_op jit(solution)/shard_map/ppermute | solution.py:252
  24.4 20.0 %collective-permute-start.5 = (bf16[400,128]{1,0:T(8,128)(2,1)S(1)}, bf16[400,128]{1,0:T(8,128)(2,1)S(1)}, u32[]{:S(2)}, u32[]{:S(2)}) collective-permute-start(bf16[400,128]{1,0:T(8,128)(2,1)S(1)} %get-tuple-element.18), channel_id=1, source_target_pairs={{0,13},{1,12},{2,15},{3,14},{4,9},{5,8},{6,11},{7,10},{8,5},{9,4},... | collective-permute-start | bytes 307208 | tf_op jit(solution)/shard_map/ppermute | solution.py:252
  27.5 21.7 %collective-permute-start.6 = (bf16[400,128]{1,0:T(8,128)(2,1)S(1)}, bf16[400,128]{1,0:T(8,128)(2,1)S(1)}, u32[]{:S(2)}, u32[]{:S(2)}) collective-permute-start(bf16[400,128]{1,0:T(8,128)(2,1)S(1)} %get-tuple-element.19), channel_id=1, source_target_pairs={{0,14},{1,15},{2,12},{3,13},{4,10},{5,11},{6,8},{7,9},{8,6},{9,7},... | collective-permute-start | bytes 307208 | tf_op jit(solution)/shard_map/ppermute | solution.py:252
  35.4 14.6 %collective-permute-start.7 = (bf16[400,128]{1,0:T(8,128)(2,1)S(1)}, bf16[400,128]{1,0:T(8,128)(2,1)S(1)}, u32[]{:S(2)}, u32[]{:S(2)}) collective-permute-start(bf16[400,128]{1,0:T(8,128)(2,1)S(1)} %get-tuple-element.20), channel_id=1, source_target_pairs={{0,15},{1,14},{2,13},{3,12},{4,11},{5,10},{6,9},{7,8},{8,7},{9,6},... | collective-permute-start | bytes 307208 | tf_op jit(solution)/shard_map/ppermute | solution.py:252
  52.2 19.6 %copy-start.6 = (f32[3,2048]{1,0:T(4,128)S(1)}, f32[3,2048]{1,0:T(4,128)}, u32[]{:S(2)}) copy-start(f32[3,2048]{1,0:T(4,128)} %gain_ref.1) | copy-start | bytes 73732
  71.9 0.7 copy-start.8

commit v3 on v0

--- a/solution.py
+++ b/solution.py
@@ -1,12 +1,21 @@
+import functools
 import math
 
 import jax
 import jax.numpy as jnp
 from jax import lax
+from jax.experimental import pallas as pl
+from jax.experimental.pallas import tpu as pltpu
 from jax.sharding import PartitionSpec as P
 
 HEADS = 16
 HEAD_DIM = 128
+CORES = 2
+TAIL = 8
+TILE = 2
+FIRST = 2
+VMEM = pl.BlockSpec(memory_space=pltpu.VMEM)
+HBM = pl.BlockSpec(memory_space=pltpu.HBM)
 
 
 def entering(part, axis, combine, identity):
@@ -53,7 +62,7 @@
     return (combined * scale).astype(jnp.bfloat16)
 
 
-def on_device(q_rows, k_rows, v_rows, block_of, modality, out_gain):
+def by_blocks(q_rows, k_rows, v_rows, block_of, modality, out_gain):
     tok_count = q_rows.shape[0]
     row_width = q_rows.shape[1]
     peer_count = lax.axis_size("seq")
@@ -102,6 +111,310 @@
     return (own_rows.astype(jnp.float32) * gains).astype(jnp.bfloat16)
 
 
+def pack_kernel(bits, q_ref, k_ref, v_ref, block_ref, mode_ref, *refs):
+    *out_refs, note_ref, sems = refs
+    rows = q_ref.shape[0]
+    width = out_refs[0].shape[1]
+    chip = lax.axis_index("seq") // CORES
+    copies = [
+        pltpu.make_async_copy(block_ref, note_ref.at[pl.ds(0, 1), :], sems.at[0]),
+        pltpu.make_async_copy(mode_ref, note_ref.at[pl.ds(8, 1), :], sems.at[1]),
+    ]
+    for bit, out_ref in zip(bits, out_refs):
+        columns = pl.ds(pl.multiple_of((chip ^ bit) * width, width), width)
+        for part, ref in enumerate((q_ref, k_ref, v_ref)):
+            place = out_ref.at[pl.ds(part * rows, rows), :]
+            copies.append(pltpu.make_async_copy(ref.at[:, columns], place, sems.at[len(copies)]))
+    for copy in copies:
+        copy.start()
+    for copy in copies:
+        copy.wait()
+    notes = jnp.concatenate([note_ref[0:1, :], note_ref[8:9, :]], axis=1).astype(jnp.float32)
+    notes = jnp.broadcast_to(notes, (TAIL, 2 * rows)).astype(out_refs[0].dtype)
+    for out_ref in out_refs:
+        out_ref[3 * rows :, :] = notes
+
+
+def pack(bits, q_rows, k_rows, v_rows, block_line, mode_line):
+    count = len(bits)
+    rows = q_rows.shape[0]
+    shape = jax.ShapeDtypeStruct((3 * rows + TAIL, CORES * HEAD_DIM), q_rows.dtype)
+    operands = [
+        pltpu.with_memory_space_constraint(x, pltpu.HBM)
+        for x in (q_rows, k_rows, v_rows, block_line, mode_line)
+    ]
+    return pl.pallas_call(
+        functools.partial(pack_kernel, bits),
+        in_specs=[HBM] * len(operands),
+        out_specs=[VMEM] * count,
+        out_shape=[shape] * count,
+        scratch_shapes=[
+            pltpu.VMEM((16, rows), jnp.int32),
+            pltpu.SemaphoreType.DMA((3 * count + 2,)),
+        ],
+        compiler_params=pltpu.CompilerParams(vmem_limit_bytes=8 << 20),
+        cost_estimate=pl.CostEstimate(flops=1 << 20, bytes_accessed=count << 18, transcendentals=0),
+    )(*operands)
+
+
+def laid_shapes(chips, rows):
+    queries = (CORES, chips * rows, HEAD_DIM)
+    keys = (CORES, CORES * chips * rows, HEAD_DIM)
+    lines = -(-CORES * chips // 8) * 8
+    return [
+        (queries, jnp.bfloat16),
+        (keys, jnp.bfloat16),
+        (keys, jnp.bfloat16),
+        ((lines, rows), jnp.float32),
+        (queries[1:], jnp.float32),
+        (queries, jnp.float32),
+    ]
+
+
+def lay(bits, direct, passed, gain_ref, q_ref, k_ref, v_ref, key_ref, column_ref, scale_ref):
+    size = q_ref.shape[2]
+    rows = q_ref.shape[1] // len(bits)
+    total = HEADS * rows
+    me = lax.axis_index("seq")
+    heads = [slice(head * size, (head + 1) * size) for head in range(CORES)]
+    modes = []
+    for i, bit in enumerate(bits):
+        for core, chunk in enumerate((direct[i], passed[i])):
+            line = CORES * i + core
+            at = slice(line * rows, (line + 1) * rows)
+            for head, lanes in enumerate(heads):
+                k_ref[head, at, :] = chunk[rows : 2 * rows, lanes]
+                v_ref[head, at, :] = chunk[2 * rows : 3 * rows, lanes]
+            notes = chunk[3 * rows : 3 * rows + TAIL, :].astype(jnp.float32)
+            source = me ^ (CORES * bit + core)
+            row_id = lax.broadcasted_iota(jnp.int32, (1, rows), 1) + source * rows
+            key_ref[line : line + 1, :] = notes[0:1, 0:rows] * total + row_id.astype(jnp.float32)
+            if core == 0:
+                modes.append(notes[0:1, rows : 2 * rows])
+        for head, lanes in enumerate(heads):
+            q_ref[head, i * rows : (i + 1) * rows, :] = direct[i][0:rows, lanes]
+    modes += [jnp.zeros((1, rows), jnp.float32)] * (-len(modes) % 8)
+    columns = key_ref[...].T
+    modes = jnp.concatenate(modes, axis=0).T
+    for i in range(len(bits)):
+        at = slice(i * rows, (i + 1) * rows)
+        line = CORES * i
+        column_ref[at, :] = jnp.broadcast_to(columns[:, line : line + 1], (rows, size))
+        mode = jnp.broadcast_to(modes[:, i : i + 1], (rows, size))
+        for head, lanes in enumerate(heads):
+            scale_ref[head, at, :] = jnp.where(
+                mode == 0.0,
+                gain_ref[0:1, lanes],
+                jnp.where(mode == 1.0, gain_ref[1:2, lanes], gain_ref[2:3, lanes]),
+            )
+
+
+def attend_tiles(total, query, column_ref, k_ref, v_ref, key_ref):
+    rows = key_ref.shape[1]
+    chunks = k_ref.shape[0] // rows
+    for first in range(0, chunks, TILE):
+        last = min(first + TILE, chunks)
+        keys = k_ref[first * rows : last * rows, :]
+        values = v_ref[first * rows : last * rows, :]
+        scores = lax.dot_general(
+            query, keys, (((1,), (1,)), ((), ())), preferred_element_type=jnp.float32
+        )
+        weights = [
+            jnp.where(
+                column_ref[...] >= key_ref[i : i + 1, :],
+                scores[:, (i - first) * rows : (i - first + 1) * rows],
+                0.0,
+            ).astype(jnp.bfloat16)
+            for i in range(first, last)
+        ]
+        part = jnp.dot(
+            jnp.concatenate(weights, axis=1), values, preferred_element_type=jnp.float32
+        )
+        total = part if total is None else total + part
+    return total
+
+
+def meet(total, head, queries, keys):
+    q_ref, _, _, _, column_ref, _ = queries
+    _, k_ref, v_ref, key_ref, _, _ = keys
+    return attend_tiles(
+        total, q_ref[head], column_ref, k_ref.at[head], v_ref.at[head], key_ref
+    )
+
+
+def finish(combined, gains):
+    scale = lax.rsqrt(jnp.mean(combined * combined, axis=-1, keepdims=True) + 1e-06)
+    normed = (combined * scale).astype(jnp.bfloat16)
+    return (normed.astype(jnp.float32) * gains).astype(jnp.bfloat16)
+
+
+def read_gain(gain_ref, held_ref, sem):
+    columns = held_ref.shape[1]
+    start = (lax.axis_index("seq") // CORES) * columns
+    window = pl.ds(pl.multiple_of(start, columns), columns)
+    copy = pltpu.make_async_copy(gain_ref.at[:, window], held_ref, sem)
+    copy.start()
+    copy.wait()
+
+
+def take_up(bits, gain_ref, refs, laid):
+    lay(bits, refs[: len(bits)], refs[len(bits) :], gain_ref, *laid)
+
+
+def stage_kernel(olds, bits, gain_ref, *refs):
+    if not olds:
+        *refs, held_ref, sem = refs
+        read_gain(gain_ref, held_ref, sem)
+        gain_ref = held_ref
+    sets = [refs[7 * i : 7 * i + 7] for i in range(olds)]
+    refs = refs[7 * olds :]
+    chunks, refs = refs[: 2 * len(bits)], refs[2 * len(bits) :]
+    sums, new_sum, laid = refs[:olds], refs[olds], refs[olds + 1 :]
+    take_up(bits, gain_ref, chunks, laid)
+    for head in range(CORES):
+        for out_ref, (sum_ref, *old) in zip(sums, sets):
+            out_ref[head] = meet(sum_ref[head], head, old, laid)
+        combined = None
+        for _, *old in sets:
+            combined = meet(combined, head, laid, old)
+        new_sum[head] = meet(combined, head, laid, laid)
+
+
+def write_back(out_refs, head, mixed):
+    rows, size = out_refs[0].shape[0], mixed.shape[1]
+    for i, out_ref in enumerate(out_refs):
+        out_ref[:, head * size : (head + 1) * size] = mixed[i * rows : (i + 1) * rows, :]
+
+
+def out_kernel(counts, bits, gain_ref, *refs):
+    sets = [refs[7 * i : 7 * i + 7] for i in range(len(counts))]
+    refs = refs[7 * len(counts) :]
+    chunks, refs = refs[: 2 * len(bits)], refs[2 * len(bits) :]
+    outs, laid = refs[:-6], refs[-6:]
+    take_up(bits, gain_ref, chunks, laid)
+    for count, (sum_ref, *old) in zip(counts, sets):
+        mine, outs = outs[:count], outs[count:]
+        for head in range(CORES):
+            combined = meet(sum_ref[head], head, old, laid)
+            write_back(mine, head, finish(combined, old[5][head]))
+    for head in range(CORES):
+        combined = None
+        for keys in [one[1:] for one in sets] + [laid]:
+            combined = meet(combined, head, laid, keys)
+        write_back(outs, head, finish(combined, laid[5][head]))
+
+
+def call(kernel, gain, operands, out_shapes, scratch_shapes, pairs, rows, read=False):
+    held = [((gain.shape[0], CORES * HEAD_DIM), jnp.float32)] if read else []
+    shapes = out_shapes + held
+    scratch = [pltpu.VMEM(*shape) for shape in scratch_shapes]
+    return list(
+        pl.pallas_call(
+            kernel,
+            in_specs=[HBM if read else VMEM] + [VMEM] * len(operands),
+            out_specs=[VMEM] * len(shapes),
+            out_shape=[jax.ShapeDtypeStruct(*shape) for shape in shapes],
+            scratch_shapes=scratch + ([pltpu.SemaphoreType.DMA(())] if read else []),
+            compiler_params=pltpu.CompilerParams(vmem_limit_bytes=24 << 20),
+            cost_estimate=pl.CostEstimate(
+                flops=8 * CORES * rows * rows * HEAD_DIM * pairs,
+                bytes_accessed=1 << 20,
+                transcendentals=0,
+            ),
+        )(gain, *operands)
+    )
+
+
+def unpack_kernel(bits, *refs):
+    *in_refs, out_ref, sems = refs
+    chip = lax.axis_index("seq") // CORES
+    copies = []
+    for i, (bit, in_ref) in enumerate(zip(bits, in_refs)):
+        width = in_ref.shape[1]
+        columns = pl.ds(pl.multiple_of((chip ^ bit) * width, width), width)
+        copies.append(pltpu.make_async_copy(in_ref, out_ref.at[:, columns], sems.at[i]))
+    for copy in copies:
+        copy.start()
+    for copy in copies:
+        copy.wait()
+
+
+def plan_of(chips):
+    half = chips // 2
+    far = list(range(half, chips))
+    near = list(range(half // 2, half)) + list(range(1, half // 2))
+    send = []
+    for i, bit in enumerate(far):
+        send += [bit] if i == len(far) - 1 else [bit] + near[i : i + 1]
+    early = far[: len(far) // 2]
+    stages = [[0, early[0], near[0]], early[1:] + near[1:], far[len(early) : -1], far[-1:]]
+    return send, stages, far[len(early) :] + early + near
+
+
+def by_heads(q_rows, k_rows, v_rows, block_of, modality, out_gain):
+    rows = q_rows.shape[0]
+    peers = lax.axis_size("seq")
+    rows_in = (q_rows, k_rows, v_rows, block_of.reshape(1, rows), modality.reshape(1, rows))
+    send, stages, order = plan_of(peers // CORES)
+
+    def across(x, bit):
+        return lax.ppermute(x, "seq", [(i, i ^ (CORES * bit)) for i in range(peers)])
+
+    sent = list(pack(send[:FIRST], *rows_in))
+    *more, own = pack(send[FIRST:] + [0], *rows_in)
+    direct, passed = {0: own}, {}
+    for bit, chunk in zip(send, sent + more):
+        direct[bit] = across(chunk, bit)
+    for bit in [bit for bits in stages for bit in bits]:
+        passed[bit] = lax.ppermute(direct[bit], "seq", [(i, i ^ 1) for i in range(peers)])
+    gain = pltpu.with_memory_space_constraint(out_gain, pltpu.HBM)
+    sets, taken = [], []
+    for number, bits in enumerate(stages):
+        last = number == len(stages) - 1
+        chunks = [direct[bit] for bit in bits] + [passed[bit] for bit in bits]
+        operands = [x for one in sets for x in one] + chunks
+        pairs = len(bits) * (2 * sum(len(one) for one in taken) + len(bits))
+        laid = laid_shapes(len(bits), rows)
+        if last:
+            counts = [len(one) for one in taken]
+            kernel = functools.partial(out_kernel, counts, bits)
+            shapes = [((rows, CORES * HEAD_DIM), q_rows.dtype)] * (sum(counts) + len(bits))
+            done = call(kernel, gain, operands, shapes, laid, pairs, rows)
+        else:
+            kernel = functools.partial(stage_kernel, len(sets), bits)
+            shapes = [(one[0].shape, jnp.float32) for one in sets]
+            shapes += [((CORES, len(bits) * rows, HEAD_DIM), jnp.float32)] + laid
+            made = call(kernel, gain, operands, shapes, [], pairs, rows, not sets)
+            if not sets:
+                gain = made.pop()
+            old = len(sets)
+            sets = [[total] + one[1:] for total, one in zip(made, sets)] + [made[old:]]
+        taken.append(bits)
+    owners = [bit for bits in taken for bit in bits]
+    done = dict(zip(owners, done))
+    for bit in order:
+        done[bit] = across(done[bit], bit)
+    back = [done[bit] for bit in owners]
+    return pl.pallas_call(
+        functools.partial(unpack_kernel, owners),
+        in_specs=[VMEM] * len(back),
+        out_specs=HBM,
+        out_shape=jax.ShapeDtypeStruct(q_rows.shape, q_rows.dtype),
+        scratch_shapes=[pltpu.SemaphoreType.DMA((len(back),))],
+        compiler_params=pltpu.CompilerParams(vmem_limit_bytes=8 << 20),
+    )(*back)
+
+
+def fits_heads(peers, rows):
+    return peers == HEADS and rows == HEAD_DIM and peers >= 16 and peers & (peers - 1) == 0
+
+
+def on_device(q_rows, k_rows, v_rows, block_of, modality, out_gain):
+    fits = fits_heads(lax.axis_size("seq"), q_rows.shape[0])
+    plan = by_heads if fits else by_blocks
+    return plan(q_rows, k_rows, v_rows, block_of, modality, out_gain)
+
+
 def solution(mesh):
     placed = (
         P(("groups", "seq"), None),

time: 288 us -> 70 us (0.24)
  the two profiles are of different devices: /device:TPU:9 before, /device:TPU:0 now
where the time goes in v3:
time: 70 us; the launch traced here: 69.8 us
  starting transfers between devices  30.6 us (44%)
  waiting for transfers between devices  27.7 us (40%)
  Pallas kernels  11.4 us (16%)
    ppermute x14, starting transfers between devices, across(): return lax.ppermute(x, 'seq', [(i, i ^ CORES * bit) for i in range(peers)])  28.9 us
    ppermute x14, waiting for transfers between devices, across(): return lax.ppermute(x, 'seq', [(i, i ^ CORES * bit) for i in range(peers)])  27.6 us
    pallas_call x4, Pallas kernels, call(): pl.pallas_call(kernel, in_specs=[HBM if read else VMEM] + [VMEM] * len(op...  7.99 us
    pallas_call x2, Pallas kernels, pack(): pl.pallas_call(functools.partial(pack_kernel, bits), in_specs=[HBM] * len...  2.6 us
    ppermute x8, starting transfers between devices, by_heads(): lax.ppermute(direct[bit], 'seq', [(i, i ^ 1) for i in range(peers)])  1.65 us
  transfers between devices with their start and end apart: 22, of which 9 were waited for; matrix products, arithmetic and copies ran while one was open for 0% of the time, Pallas kernels for 10%

profile of v3, /device:TPU:0, one launch (start us, length us, event | category | flops | bytes accessed | tf_op | source)
XLA Modules:
  0.0 69.8 jit_solution(17808505867969928902)
XLA Ops:
  0.0 1.5 %shard_map.64 = (bf16[392,256]{1,0:T(8,128)(2,1)S(1)}, bf16[392,256]{1,0:T(8,128)(2,1)S(1)}, bf16[392,256]{1,0:T(8,128)(2,1)S(1)}, bf16[392,256]{1,0:T(8,128)(2,...) custom-call(bf16[128,2048]{1,0:T(8,128)(2,1)} %q_ref.3, bf16[128,2048]{1,0:T(8,128)(2,1)} %k_ref.3, ...), custom_call_target="tpu_custom_call" | custom-call | flops 1048576 | bytes 1572864 | tf_op jit(solution)/shard_map/pallas_call | solution.py:146
  2.1 1.1 %shard_map.65 = (bf16[392,256]{1,0:T(8,128)(2,1)S(1)}, bf16[392,256]{1,0:T(8,128)(2,1)S(1)}) custom-call(bf16[128,2048]{1,0:T(8,128)(2,1)} %q_ref.3, bf16[128,2048]{1,0:T(8,128)(2,1)} %k_ref.3, bf16[128,2048]{1,0:T(8,128)(2,1)} %v_ref.3, s32[1,128]{1,0:T(1,128)} %bitcast.3, s32[1,128]{1,0:T(1,128)} %bitcast.5), custom_call_target="tpu_custom_call" | custom-call | flops 1048576 | bytes 524288 | tf_op jit(solution)/shard_map/pallas_call | solution.py:146
  3.2 3.7 %collective-permute-start = (bf16[392,256]{1,0:T(8,128)(2,1)S(1)}, bf16[392,256]{1,0:T(8,128)(2,1)S(1)}, u32[]{:S(2)}, u32[]{:S(2)}) collective-permute-start(bf16[392,256]{1,0:T(8,128)(2,1)S(1)} %get-tuple-element.47), channel_id=1, source_target_pairs={{0,8},{1,9},{2,10},{3,11},{4,12},{5,13},{6,14},{7,15},{8,0},{9,1},... | collective-permute-start | bytes 602120 | tf_op jit(solution)/shard_map/ppermute | solution.py:361
  6.8 1.6 %collective-permute-start.1 = (bf16[392,256]{1,0:T(8,128)(2,1)S(1)}, bf16[392,256]{1,0:T(8,128)(2,1)S(1)}, u32[]{:S(2)}, u32[]{:S(2)}) collective-permute-start(bf16[392,256]{1,0:T(8,128)(2,1)S(1)} %get-tuple-element.48), channel_id=1, source_target_pairs={{0,4},{1,5},{2,6},{3,7},{4,0},{5,1},{6,2},{7,3},{8,12},{9,13},{10,... | collective-permute-start | bytes 602120 | tf_op jit(solution)/shard_map/ppermute | solution.py:361
  8.4 1.5 %collective-permute-start.7 = (bf16[392,256]{1,0:T(8,128)(2,1)S(1)}, bf16[392,256]{1,0:T(8,128)(2,1)S(1)}, u32[]{:S(2)}, u32[]{:S(2)}) collective-permute-start(bf16[392,256]{1,0:T(8,128)(2,1)S(1)} %get-tuple-element.59), channel_id=1, source_target_pairs={{0,2},{1,3},{2,0},{3,1},{4,6},{5,7},{6,4},{7,5},{8,10},{9,11},{10,... | collective-permute-start | bytes 602120 | tf_op jit(solution)/shard_map/ppermute | solution.py:361
  10.2 1.4 %collective-permute-start.6 = (bf16[392,256]{1,0:T(8,128)(2,1)S(1)}, bf16[392,256]{1,0:T(8,128)(2,1)S(1)}, u32[]{:S(2)}, u32[]{:S(2)}) collective-permute-start(bf16[392,256]{1,0:T(8,128)(2,1)S(1)} %get-tuple-element.58), channel_id=1, source_target_pairs={{0,6},{1,7},{2,4},{3,5},{4,2},{5,3},{6,0},{7,1},{8,14},{9,15},{10,... | collective-permute-start | bytes 602120 | tf_op jit(solution)/shard_map/ppermute | solution.py:361
  11.6 5.5 %collective-permute-done.refs_1_ = bf16[392,256]{1,0:T(8,128)(2,1)S(1)} collective-permute-done((bf16[392,256]{1,0:T(8,128)(2,1)S(1)}, bf16[392,256]{1,0:T(8,128)(2,1)S(1)}, u32[]{:S(2)}, u32[]{:S(2)}) %collective-permute-start) | collective-permute-done | bytes 200736 | tf_op jit(solution)/shard_map/ppermute | solution.py:361
  17.1 3.8 %collective-permute-start.11 = (bf16[392,256]{1,0:T(8,128)(2,1)S(1)}, bf16[392,256]{1,0:T(8,128)(2,1)S(1)}, u32[]{:S(2)}, u32[]{:S(2)}) collective-permute-start(bf16[392,256]{1,0:T(8,128)(2,1)S(1)} %get-tuple-element.68), channel_id=1, source_target_pairs={{0,12},{1,13},{2,14},{3,15},{4,8},{5,9},{6,10},{7,11},{8,4},{9,5},... | collective-permute-start | bytes 602120 | tf_op jit(solution)/shard_map/ppermute | solution.py:361
  20.9 1.3 %collective-permute-start.13 = (bf16[392,256]{1,0:T(8,128)(2,1)S(1)}, bf16[392,256]{1,0:T(8,128)(2,1)S(1)}, u32[]{:S(2)}, u32[]{:S(2)}) collective-permute-start(bf16[392,256]{1,0:T(8,128)(2,1)S(1)} %get-tuple-element.78), channel_id=1, source_target_pairs={{0,14},{1,15},{2,12},{3,13},{4,10},{5,11},{6,8},{7,9},{8,6},{9,7},... | collective-permute-start | bytes 602120 | tf_op jit(solution)/shard_map/ppermute | solution.py:361
  22.2 4.8 %collective-permute-done.5.refs_7_ = bf16[392,256]{1,0:T(8,128)(2,1)S(1)} collective-permute-done((bf16[392,256]{1,0:T(8,128)(2,1)S(1)}, bf16[392,256]{1,0:T(8,128)(2,1)S(1)}, u32[]{:S(2)}, u32[]{:S(2)}) %collective-permute-start.5) | collective-permute-done | bytes 200736 | tf_op jit(solution)/shard_map/ppermute | solution.py:361
  27.5 5.0 %collective-permute-done.11.refs_14_ = bf16[392,256]{1,0:T(8,128)(2,1)S(1)} collective-permute-done((bf16[392,256]{1,0:T(8,128)(2,1)S(1)}, bf16[392,256]{1,0:T(8,128)(2,1)S(1)}, u32[]{:S(2)}, u32[]{:S(2)}) %collective-permute-start.11) | collective-permute-done | bytes 200736 | tf_op jit(solution)/shard_map/ppermute | solution.py:361
  32.4 4.8 %collective-permute-done.13.refs_21_ = bf16[392,256]{1,0:T(8,128)(2,1)S(1)} collective-permute-done((bf16[392,256]{1,0:T(8,128)(2,1)S(1)}, bf16[392,256]{1,0:T(8,128)(2,1)S(1)}, u32[]{:S(2)}, u32[]{:S(2)}) %collective-permute-start.13) | collective-permute-done | bytes 200736 | tf_op jit(solution)/shard_map/ppermute | solution.py:361
  37.8 1.8 %shard_map.66 = (f32[2,384,128]{2,1,0:T(8,128)S(1)}, bf16[2,384,128]{2,1,0:T(8,128)(2,1)S(1)}, bf16[2,768,128]{2,1,0:T(8,128)(2,1)S(1)}, bf16[2,768,128]{2,1,0:T...) custom-call(f32[3,2048]{1,0:T(4,128)} %gain_ref.1, ...), custom_call_target="tpu_custom_call" | custom-call | flops 301989888 | bytes 1048576 | tf_op jit(solution)/shard_map/pallas_call | solution.py:312
  39.7 2.6 %shard_map.67 = (f32[2,384,128]{2,1,0:T(8,128)S(1)}, f32[2,384,128]{2,1,0:T(8,128)S(1)}, bf16[2,384,128]{2,1,0:T(8,128)(2,1)S(1)}, bf16[2,768,128]{2,1,0:T(8,128...) custom-call(f32[3,256]{1,0:T(4,128)S(1)} %get-tuple-element.49.gain_, ...), custom_call_target="tpu_custom_call" | custom-call | flops 905969664 | bytes 1048576 | tf_op jit(solution)/shard_map/pallas_call | solution.py:312
  42.3 1.6 %shard_map.68 = (f32[2,384,128]{2,1,0:T(8,128)S(1)}, f32[2,384,128]{2,1,0:T(8,128)S(1)}, f32[2,128,128]{2,1,0:T(8,128)S(1)}, bf16[2,128,128]{2,1,0:T(8,128)(2,1)...) custom-call(f32[3,256]{1,0:T(4,128)S(1)} %get-tuple-element.49.gain_, ...), custom_call_target="tpu_custom_call" | custom-call | flops 436207616 | bytes 1048576 | tf_op jit(solution)/shard_map/pallas_call | solution.py:312
  44.0 1.9 %shard_map.69 = (bf16[128,256]{1,0:T(8,128)(2,1)S(1)}, bf16[128,256]{1,0:T(8,128)(2,1)S(1)}, bf16[128,256]{1,0:T(8,128)(2,1)S(1)}, bf16[128,256]{1,0:T(8,128)(2,...) custom-call(f32[3,256]{1,0:T(4,128)S(1)} %get-tuple-element.49.gain_, ...), custom_call_target="tpu_custom_call" | custom-call | flops 503316480 | bytes 1048576 | tf_op jit(solution)/shard_map/pallas_call | solution.py:312
  45.9 9.1 %collective-permute-start.15 = (bf16[128,256]{1,0:T(8,128)(2,1)S(1)}, bf16[128,256]{1,0:T(8,128)(2,1)S(1)}, u32[]{:S(2)}, u32[]{:S(2)}) collective-permute-start(bf16[128,256]{1,0:T(8,128)(2,1)S(1)} %get-tuple-element.80), channel_id=1, source_target_pairs={{0,8},{1,9},{2,10},{3,11},{4,12},{5,13},{6,14},{7,15},{8,0},{9,1},... | collective-permute-start | bytes 196616 | tf_op jit(solution)/shard_map/ppermute | solution.py:361
  55.0 1.0 %collective-permute-start.17 = (bf16[128,256]{1,0:T(8,128)(2,1)S(1)}, bf16[128,256]{1,0:T(8,128)(2,1)S(1)}, u32[]{:S(2)}, u32[]{:S(2)}) collective-permute-start(bf16[128,256]{1,0:T(8,128)(2,1)S(1)} %get-tuple-element.82), channel_id=1, source_target_pairs={{0,10},{1,11},{2,8},{3,9},{4,14},{5,15},{6,12},{7,13},{8,2},{9,3},... | collective-permute-start | bytes 196616 | tf_op jit(solution)/shard_map/ppermute | solution.py:361
  56.0 2.0 %collective-permute-start.18 = (bf16[128,256]{1,0:T(8,128)(2,1)S(1)}, bf16[128,256]{1,0:T(8,128)(2,1)S(1)}, u32[]{:S(2)}, u32[]{:S(2)}) collective-permute-start(bf16[128,256]{1,0:T(8,128)(2,1)S(1)} %get-tuple-element.83), channel_id=1, source_target_pairs={{0,6},{1,7},{2,4},{3,5},{4,2},{5,3},{6,0},{7,1},{8,14},{9,15},{10,... | collective-permute-start | bytes 196616 | tf_op jit(solution)/shard_map/ppermute | solution.py:361
  59.3 1.5 %collective-permute-start.20 = (bf16[128,256]{1,0:T(8,128)(2,1)S(1)}, bf16[128,256]{1,0:T(8,128)(2,1)S(1)}, u32[]{:S(2)}, u32[]{:S(2)}) collective-permute-start(bf16[128,256]{1,0:T(8,128)(2,1)S(1)} %get-tuple-element.85), channel_id=1, source_target_pairs={{0,12},{1,13},{2,14},{3,15},{4,8},{5,9},{6,10},{7,11},{8,4},{9,5},... | collective-permute-start | bytes 196616 | tf_op jit(solution)/shard_map/ppermute | solution.py:361
  60.8 1.1 %collective-permute-done.16.refs_2_ = bf16[128,256]{1,0:T(8,128)(2,1)S(1)} collective-permute-done((bf16[128,256]{1,0:T(8,128)(2,1)S(1)}, bf16[128,256]{1,0:T(8,128)(2,1)S(1)}, u32[]{:S(2)}, u32[]{:S(2)}) %collective-permute-start.16) | collective-permute-done | bytes 65568 | tf_op jit(solution)/shard_map/ppermute | solution.py:361
  61.9 1.3 %collective-permute-start.21 = (bf16[128,256]{1,0:T(8,128)(2,1)S(1)}, bf16[128,256]{1,0:T(8,128)(2,1)S(1)}, u32[]{:S(2)}, u32[]{:S(2)}) collective-permute-start(bf16[128,256]{1,0:T(8,128)(2,1)S(1)} %get-tuple-element.86), channel_id=1, source_target_pairs={{0,14},{1,15},{2,12},{3,13},{4,10},{5,11},{6,8},{7,9},{8,6},{9,7},... | collective-permute-start | bytes 196616 | tf_op jit(solution)/shard_map/ppermute | solution.py:361
  63.7 1.9 %collective-permute-done.20.refs_6_ = bf16[128,256]{1,0:T(8,128)(2,1)S(1)} collective-permute-done((bf16[128,256]{1,0:T(8,128)(2,1)S(1)}, bf16[128,256]{1,0:T(8,128)(2,1)S(1)}, u32[]{:S(2)}, u32[]{:S(2)}) %collective-permute-start.20) | collective-permute-done | bytes 65568 | tf_op jit(solution)/shard_map/ppermute | solution.py:361
  65.6 3.3 %collective-permute-done.21.refs_7_ = bf16[128,256]{1,0:T(8,128)(2,1)S(1)} collective-permute-done((bf16[128,256]{1,0:T(8,128)(2,1)S(1)}, bf16[128,256]{1,0:T(8,128)(2,1)S(1)}, u32[]{:S(2)}, u32[]{:S(2)}) %collective-permute-start.21) | collective-permute-done | bytes 65568 | tf_op jit(solution)/shard_map/ppermute | solution.py:361
  (27 shorter events, 4.7 us)
Async XLA Ops:
  1.5 8.7 %collective-permute-start.2 = (bf16[392,256]{1,0:T(8,128)(2,1)S(1)}, bf16[392,256]{1,0:T(8,128)(2,1)S(1)}, u32[]{:S(2)}, u32[]{:S(2)}) collective-permute-start(bf16[392,256]{1,0:T(8,128)(2,1)S(1)} %get-tuple-element.46.refs_0_), channel_id=1, source_target_pairs={{0,1},{1,0},{2,3},{3,2},{4,5},{5,4},{6,7},{7,6},{8,9},{9,8},{10,11... | collective-permute-start | bytes 602120 | tf_op jit(solution)/shard_map/ppermute | solution.py:369
  3.2 13.9 %collective-permute-start = (bf16[392,256]{1,0:T(8,128)(2,1)S(1)}, bf16[392,256]{1,0:T(8,128)(2,1)S(1)}, u32[]{:S(2)}, u32[]{:S(2)}) collective-permute-start(bf16[392,256]{1,0:T(8,128)(2,1)S(1)} %get-tuple-element.47), channel_id=1, source_target_pairs={{0,8},{1,9},{2,10},{3,11},{4,12},{5,13},{6,14},{7,15},{8,0},{9,1},... | collective-permute-start | bytes 602120 | tf_op jit(solution)/shard_map/ppermute | solution.py:361
  6.8 14.1 %collective-permute-start.1 = (bf16[392,256]{1,0:T(8,128)(2,1)S(1)}, bf16[392,256]{1,0:T(8,128)(2,1)S(1)}, u32[]{:S(2)}, u32[]{:S(2)}) collective-permute-start(bf16[392,256]{1,0:T(8,128)(2,1)S(1)} %get-tuple-element.48), channel_id=1, source_target_pairs={{0,4},{1,5},{2,6},{3,7},{4,0},{5,1},{6,2},{7,3},{8,12},{9,13},{10,... | collective-permute-start | bytes 602120 | tf_op jit(solution)/shard_map/ppermute | solution.py:361
  8.4 13.8 %collective-permute-start.7 = (bf16[392,256]{1,0:T(8,128)(2,1)S(1)}, bf16[392,256]{1,0:T(8,128)(2,1)S(1)}, u32[]{:S(2)}, u32[]{:S(2)}) collective-permute-start(bf16[392,256]{1,0:T(8,128)(2,1)S(1)} %get-tuple-element.59), channel_id=1, source_target_pairs={{0,2},{1,3},{2,0},{3,1},{4,6},{5,7},{6,4},{7,5},{8,10},{9,11},{10,... | collective-permute-start | bytes 602120 | tf_op jit(solution)/shard_map/ppermute | solution.py:361
  9.9 17.0 %collective-permute-start.5 = (bf16[392,256]{1,0:T(8,128)(2,1)S(1)}, bf16[392,256]{1,0:T(8,128)(2,1)S(1)}, u32[]{:S(2)}, u32[]{:S(2)}) collective-permute-start(bf16[392,256]{1,0:T(8,128)(2,1)S(1)} %get-tuple-element.57), channel_id=1, source_target_pairs={{0,10},{1,11},{2,8},{3,9},{4,14},{5,15},{6,12},{7,13},{8,2},{9,3},... | collective-permute-start | bytes 602120 | tf_op jit(solution)/shard_map/ppermute | solution.py:361
  10.2 16.7 %collective-permute-start.6 = (bf16[392,256]{1,0:T(8,128)(2,1)S(1)}, bf16[392,256]{1,0:T(8,128)(2,1)S(1)}, u32[]{:S(2)}, u32[]{:S(2)}) collective-permute-start(bf16[392,256]{1,0:T(8,128)(2,1)S(1)} %get-tuple-element.58), channel_id=1, source_target_pairs={{0,6},{1,7},{2,4},{3,5},{4,2},{5,3},{6,0},{7,1},{8,14},{9,15},{10,... | collective-permute-start | bytes 602120 | tf_op jit(solution)/shard_map/ppermute | solution.py:361
  17.1 15.3 %collective-permute-start.11 = (bf16[392,256]{1,0:T(8,128)(2,1)S(1)}, bf16[392,256]{1,0:T(8,128)(2,1)S(1)}, u32[]{:S(2)}, u32[]{:S(2)}) collective-permute-start(bf16[392,256]{1,0:T(8,128)(2,1)S(1)} %get-tuple-element.68), channel_id=1, source_target_pairs={{0,12},{1,13},{2,14},{3,15},{4,8},{5,9},{6,10},{7,11},{8,4},{9,5},... | collective-permute-start | bytes 602120 | tf_op jit(solution)/shard_map/ppermute | solution.py:361
  20.9 16.3 %collective-permute-start.13 = (bf16[392,256]{1,0:T(8,128)(2,1)S(1)}, bf16[392,256]{1,0:T(8,128)(2,1)S(1)}, u32[]{:S(2)}, u32[]{:S(2)}) collective-permute-start(bf16[392,256]{1,0:T(8,128)(2,1)S(1)} %get-tuple-element.78), channel_id=1, source_target_pairs={{0,14},{1,15},{2,12},{3,13},{4,10},{5,11},{6,8},{7,9},{8,6},{9,7},... | collective-permute-start | bytes 602120 | tf_op jit(solution)/shard_map/ppermute | solution.py:361
  22.2 15.0 %collective-permute-start.3 = (bf16[392,256]{1,0:T(8,128)(2,1)S(1)}, bf16[392,256]{1,0:T(8,128)(2,1)S(1)}, u32[]{:S(2)}, u32[]{:S(2)}) collective-permute-start(bf16[392,256]{1,0:T(8,128)(2,1)S(1)} %collective-permute-done.refs_1_), channel_id=1, source_target_pairs={{0,1},{1,0},{2,3},{3,2},{4,5},{5,4},{6,7},{7,6},{8,9},{9,8},{10,11... | collective-permute-start | bytes 602120 | tf_op jit(solution)/shard_map/ppermute | solution.py:369
  27.0 10.8 %collective-permute-start.4 = (bf16[392,256]{1,0:T(8,128)(2,1)S(1)}, bf16[392,256]{1,0:T(8,128)(2,1)S(1)}, u32[]{:S(2)}, u32[]{:S(2)}) collective-permute-start(bf16[392,256]{1,0:T(8,128)(2,1)S(1)} %collective-permute-done.1.refs_2_), channel_id=1, source_target_pairs={{0,1},{1,0},{2,3},{3,2},{4,5},{5,4},{6,7},{7,6},{8,9},{9,8},{10,11... | collective-permute-start | bytes 602120 | tf_op jit(solution)/shard_map/ppermute | solution.py:369
  27.0 12.7 %collective-permute-start.10 = (bf16[392,256]{1,0:T(8,128)(2,1)S(1)}, bf16[392,256]{1,0:T(8,128)(2,1)S(1)}, u32[]{:S(2)}, u32[]{:S(2)}) collective-permute-start(bf16[392,256]{1,0:T(8,128)(2,1)S(1)} %collective-permute-done.7.refs_9_), channel_id=1, source_target_pairs={{0,1},{1,0},{2,3},{3,2},{4,5},{5,4},{6,7},{7,6},{8,9},{9,8},{10,11... | collective-permute-start | bytes 602120 | tf_op jit(solution)/shard_map/ppermute | solution.py:369
  32.4 7.2 %collective-permute-start.8 = (bf16[392,256]{1,0:T(8,128)(2,1)S(1)}, bf16[392,256]{1,0:T(8,128)(2,1)S(1)}, u32[]{:S(2)}, u32[]{:S(2)}) collective-permute-start(bf16[392,256]{1,0:T(8,128)(2,1)S(1)} %collective-permute-done.5.refs_7_), channel_id=1, source_target_pairs={{0,1},{1,0},{2,3},{3,2},{4,5},{5,4},{6,7},{7,6},{8,9},{9,8},{10,11... | collective-permute-start | bytes 602120 | tf_op jit(solution)/shard_map/ppermute | solution.py:369
  37.2 2.5 %collective-permute-start.9 = (bf16[392,256]{1,0:T(8,128)(2,1)S(1)}, bf16[392,256]{1,0:T(8,128)(2,1)S(1)}, u32[]{:S(2)}, u32[]{:S(2)}) collective-permute-start(bf16[392,256]{1,0:T(8,128)(2,1)S(1)} %collective-permute-done.6.refs_8_), channel_id=1, source_target_pairs={{0,1},{1,0},{2,3},{3,2},{4,5},{5,4},{6,7},{7,6},{8,9},{9,8},{10,11... | collective-permute-start | bytes 602120 | tf_op jit(solution)/shard_map/ppermute | solution.py:369
  37.2 5.1 %collective-permute-start.12 = (bf16[392,256]{1,0:T(8,128)(2,1)S(1)}, bf16[392,256]{1,0:T(8,128)(2,1)S(1)}, u32[]{:S(2)}, u32[]{:S(2)}) collective-permute-start(bf16[392,256]{1,0:T(8,128)(2,1)S(1)} %collective-permute-done.11.refs_14_), channel_id=1, source_target_pairs={{0,1},{1,0},{2,3},{3,2},{4,5},{5,4},{6,7},{7,6},{8,9},{9,8},{10,11... | collective-permute-start | bytes 602120 | tf_op jit(solution)/shard_map/ppermute | solution.py:369
  37.7 6.2 %collective-permute-start.14 = (bf16[392,256]{1,0:T(8,128)(2,1)S(1)}, bf16[392,256]{1,0:T(8,128)(2,1)S(1)}, u32[]{:S(2)}, u32[]{:S(2)}) collective-permute-start(bf16[392,256]{1,0:T(8,128)(2,1)S(1)} %collective-permute-done.13.refs_21_), channel_id=1, source_target_pairs={{0,1},{1,0},{2,3},{3,2},{4,5},{5,4},{6,7},{7,6},{8,9},{9,8},{10,11... | collective-permute-start | bytes 602120 | tf_op jit(solution)/shard_map/ppermute | solution.py:369
  45.9 13.5 %collective-permute-start.15 = (bf16[128,256]{1,0:T(8,128)(2,1)S(1)}, bf16[128,256]{1,0:T(8,128)(2,1)S(1)}, u32[]{:S(2)}, u32[]{:S(2)}) collective-permute-start(bf16[128,256]{1,0:T(8,128)(2,1)S(1)} %get-tuple-element.80), channel_id=1, source_target_pairs={{0,8},{1,9},{2,10},{3,11},{4,12},{5,13},{6,14},{7,15},{8,0},{9,1},... | collective-permute-start | bytes 196616 | tf_op jit(solution)/shard_map/ppermute | solution.py:361
  54.9 7.0 %collective-permute-start.16 = (bf16[128,256]{1,0:T(8,128)(2,1)S(1)}, bf16[128,256]{1,0:T(8,128)(2,1)S(1)}, u32[]{:S(2)}, u32[]{:S(2)}) collective-permute-start(bf16[128,256]{1,0:T(8,128)(2,1)S(1)} %get-tuple-element.81), channel_id=1, source_target_pairs={{0,4},{1,5},{2,6},{3,7},{4,0},{5,1},{6,2},{7,3},{8,12},{9,13},{10,... | collective-permute-start | bytes 196616 | tf_op jit(solution)/shard_map/ppermute | solution.py:361
  55.0 8.3 %collective-permute-start.17 = (bf16[128,256]{1,0:T(8,128)(2,1)S(1)}, bf16[128,256]{1,0:T(8,128)(2,1)S(1)}, u32[]{:S(2)}, u32[]{:S(2)}) collective-permute-start(bf16[128,256]{1,0:T(8,128)(2,1)S(1)} %get-tuple-element.82), channel_id=1, source_target_pairs={{0,10},{1,11},{2,8},{3,9},{4,14},{5,15},{6,12},{7,13},{8,2},{9,3},... | collective-permute-start | bytes 196616 | tf_op jit(solution)/shard_map/ppermute | solution.py:361
  56.0 7.3 %collective-permute-start.18 = (bf16[128,256]{1,0:T(8,128)(2,1)S(1)}, bf16[128,256]{1,0:T(8,128)(2,1)S(1)}, u32[]{:S(2)}, u32[]{:S(2)}) collective-permute-start(bf16[128,256]{1,0:T(8,128)(2,1)S(1)} %get-tuple-element.83), channel_id=1, source_target_pairs={{0,6},{1,7},{2,4},{3,5},{4,2},{5,3},{6,0},{7,1},{8,14},{9,15},{10,... | collective-permute-start | bytes 196616 | tf_op jit(solution)/shard_map/ppermute | solution.py:361
  58.0 5.8 %collective-permute-start.19 = (bf16[128,256]{1,0:T(8,128)(2,1)S(1)}, bf16[128,256]{1,0:T(8,128)(2,1)S(1)}, u32[]{:S(2)}, u32[]{:S(2)}) collective-permute-start(bf16[128,256]{1,0:T(8,128)(2,1)S(1)} %get-tuple-element.84), channel_id=1, source_target_pairs={{0,2},{1,3},{2,0},{3,1},{4,6},{5,7},{6,4},{7,5},{8,10},{9,11},{10,... | collective-permute-start | bytes 196616 | tf_op jit(solution)/shard_map/ppermute | solution.py:361
  59.3 6.3 %collective-permute-start.20 = (bf16[128,256]{1,0:T(8,128)(2,1)S(1)}, bf16[128,256]{1,0:T(8,128)(2,1)S(1)}, u32[]{:S(2)}, u32[]{:S(2)}) collective-permute-start(bf16[128,256]{1,0:T(8,128)(2,1)S(1)} %get-tuple-element.85), channel_id=1, source_target_pairs={{0,12},{1,13},{2,14},{3,15},{4,8},{5,9},{6,10},{7,11},{8,4},{9,5},... | collective-permute-start | bytes 196616 | tf_op jit(solution)/shard_map/ppermute | solution.py:361
  61.9 7.0 %collective-permute-start.21 = (bf16[128,256]{1,0:T(8,128)(2,1)S(1)}, bf16[128,256]{1,0:T(8,128)(2,1)S(1)}, u32[]{:S(2)}, u32[]{:S(2)}) collective-permute-start(bf16[128,256]{1,0:T(8,128)(2,1)S(1)} %get-tuple-element.86), channel_id=1, source_target_pairs={{0,14},{1,15},{2,12},{3,13},{4,10},{5,11},{6,8},{7,9},{8,6},{9,7},... | collective-permute-start | bytes 196616 | tf_op jit(solution)/shard_map/ppermute | solution.py:361

commit v4 on v3

--- a/solution.py
+++ b/solution.py
@@ -111,49 +111,57 @@
     return (own_rows.astype(jnp.float32) * gains).astype(jnp.bfloat16)
 
 
-def pack_kernel(bits, q_ref, k_ref, v_ref, block_ref, mode_ref, *refs):
+def pack_kernel(jobs, q_ref, k_ref, v_ref, block_ref, mode_ref, *refs):
     *out_refs, note_ref, sems = refs
     rows = q_ref.shape[0]
     width = out_refs[0].shape[1]
     chip = lax.axis_index("seq") // CORES
+    source = {"q": q_ref, "k": k_ref, "v": v_ref}
     copies = [
         pltpu.make_async_copy(block_ref, note_ref.at[pl.ds(0, 1), :], sems.at[0]),
         pltpu.make_async_copy(mode_ref, note_ref.at[pl.ds(8, 1), :], sems.at[1]),
     ]
-    for bit, out_ref in zip(bits, out_refs):
+    for (bit, parts), out_ref in zip(jobs, out_refs):
         columns = pl.ds(pl.multiple_of((chip ^ bit) * width, width), width)
-        for part, ref in enumerate((q_ref, k_ref, v_ref)):
+        for part, name in enumerate(parts):
             place = out_ref.at[pl.ds(part * rows, rows), :]
-            copies.append(pltpu.make_async_copy(ref.at[:, columns], place, sems.at[len(copies)]))
+            copies.append(
+                pltpu.make_async_copy(source[name].at[:, columns], place, sems.at[len(copies)])
+            )
     for copy in copies:
         copy.start()
     for copy in copies:
         copy.wait()
     notes = jnp.concatenate([note_ref[0:1, :], note_ref[8:9, :]], axis=1).astype(jnp.float32)
     notes = jnp.broadcast_to(notes, (TAIL, 2 * rows)).astype(out_refs[0].dtype)
-    for out_ref in out_refs:
-        out_ref[3 * rows :, :] = notes
-
-
-def pack(bits, q_rows, k_rows, v_rows, block_line, mode_line):
-    count = len(bits)
+    for (_, parts), out_ref in zip(jobs, out_refs):
+        if "k" in parts:
+            out_ref[len(parts) * rows :, :] = notes
+
+
+def pack(jobs, q_rows, k_rows, v_rows, block_line, mode_line):
     rows = q_rows.shape[0]
-    shape = jax.ShapeDtypeStruct((3 * rows + TAIL, CORES * HEAD_DIM), q_rows.dtype)
+    shapes = [
+        jax.ShapeDtypeStruct(
+            (len(parts) * rows + TAIL * ("k" in parts), CORES * HEAD_DIM), q_rows.dtype
+        )
+        for _, parts in jobs
+    ]
     operands = [
         pltpu.with_memory_space_constraint(x, pltpu.HBM)
         for x in (q_rows, k_rows, v_rows, block_line, mode_line)
     ]
+    count = sum(len(parts) for _, parts in jobs) + 2
     return pl.pallas_call(
-        functools.partial(pack_kernel, bits),
+        functools.partial(pack_kernel, jobs),
         in_specs=[HBM] * len(operands),
-        out_specs=[VMEM] * count,
-        out_shape=[shape] * count,
-        scratch_shapes=[
-            pltpu.VMEM((16, rows), jnp.int32),
-            pltpu.SemaphoreType.DMA((3 * count + 2,)),
-        ],
+        out_specs=[VMEM] * len(jobs),
+        out_shape=shapes,
+        scratch_shapes=[pltpu.VMEM((16, rows), jnp.int32), pltpu.SemaphoreType.DMA((count,))],
         compiler_params=pltpu.CompilerParams(vmem_limit_bytes=8 << 20),
-        cost_estimate=pl.CostEstimate(flops=1 << 20, bytes_accessed=count << 18, transcendentals=0),
+        cost_estimate=pl.CostEstimate(
+            flops=1 << 20, bytes_accessed=len(jobs) << 18, transcendentals=0
+        ),
     )(*operands)
 
 
@@ -182,17 +190,19 @@
         for core, chunk in enumerate((direct[i], passed[i])):
             line = CORES * i + core
             at = slice(line * rows, (line + 1) * rows)
+            tail = chunk.shape[0] - TAIL
             for head, lanes in enumerate(heads):
-                k_ref[head, at, :] = chunk[rows : 2 * rows, lanes]
-                v_ref[head, at, :] = chunk[2 * rows : 3 * rows, lanes]
-            notes = chunk[3 * rows : 3 * rows + TAIL, :].astype(jnp.float32)
+                k_ref[head, at, :] = chunk[tail - 2 * rows : tail - rows, lanes]
+                v_ref[head, at, :] = chunk[tail - rows : tail, lanes]
+            notes = chunk[tail : tail + TAIL, :].astype(jnp.float32)
             source = me ^ (CORES * bit + core)
             row_id = lax.broadcasted_iota(jnp.int32, (1, rows), 1) + source * rows
             key_ref[line : line + 1, :] = notes[0:1, 0:rows] * total + row_id.astype(jnp.float32)
             if core == 0:
                 modes.append(notes[0:1, rows : 2 * rows])
-        for head, lanes in enumerate(heads):
-            q_ref[head, i * rows : (i + 1) * rows, :] = direct[i][0:rows, lanes]
+        if direct[i].shape[0] > 3 * rows:
+            for head, lanes in enumerate(heads):
+                q_ref[head, i * rows : (i + 1) * rows, :] = direct[i][0:rows, lanes]
     modes += [jnp.zeros((1, rows), jnp.float32)] * (-len(modes) % 8)
     columns = key_ref[...].T
     modes = jnp.concatenate(modes, axis=0).T
@@ -286,21 +296,46 @@
         out_ref[:, head * size : (head + 1) * size] = mixed[i * rows : (i + 1) * rows, :]
 
 
-def out_kernel(counts, bits, gain_ref, *refs):
-    sets = [refs[7 * i : 7 * i + 7] for i in range(len(counts))]
-    refs = refs[7 * len(counts) :]
-    chunks, refs = refs[: 2 * len(bits)], refs[2 * len(bits) :]
-    outs, laid = refs[:-6], refs[-6:]
-    take_up(bits, gain_ref, chunks, laid)
-    for count, (sum_ref, *old) in zip(counts, sets):
-        mine, outs = outs[:count], outs[count:]
+def rest_kernel(picks, olds, bits, gain_ref, *refs):
+    sets = [refs[7 * i : 7 * i + 7] for i in range(olds)]
+    refs = refs[7 * olds :]
+    count = sum(high - low for _, low, high in picks)
+    if bits:
+        chunks, refs = refs[: 2 * len(bits)], refs[2 * len(bits) :]
+        outs, laid = refs[:count], refs[count:]
+        take_up(bits, gain_ref, chunks, laid)
+    else:
+        laid, outs = refs[:6], refs[6:]
+    rows = outs[0].shape[0]
+    _, k_ref, v_ref, key_ref, _, _ = laid
+    for place, low, high in picks:
+        sum_ref, q_ref, _, _, _, column_ref, scale_ref = sets[place]
+        mine, outs = outs[: high - low], outs[high - low :]
+        part = slice(low * rows, high * rows)
         for head in range(CORES):
-            combined = meet(sum_ref[head], head, old, laid)
-            write_back(mine, head, finish(combined, old[5][head]))
+            combined = attend_tiles(
+                sum_ref[head, part, :],
+                q_ref[head, part, :],
+                column_ref.at[part, :],
+                k_ref.at[head],
+                v_ref.at[head],
+                key_ref,
+            )
+            write_back(mine, head, finish(combined, scale_ref[head, part, :]))
+
+
+def new_kernel(olds, query_ref, *refs):
+    laid, refs = refs[:6], refs[6:]
+    sets = [refs[7 * i + 1 : 7 * i + 7] for i in range(olds)]
+    outs = refs[7 * olds :]
+    size = laid[1].shape[2]
     for head in range(CORES):
+        query = query_ref[:, head * size : (head + 1) * size]
         combined = None
-        for keys in [one[1:] for one in sets] + [laid]:
-            combined = meet(combined, head, laid, keys)
+        for _, k_ref, v_ref, key_ref, _, _ in sets + [laid]:
+            combined = attend_tiles(
+                combined, query, laid[4], k_ref.at[head], v_ref.at[head], key_ref
+            )
         write_back(outs, head, finish(combined, laid[5][head]))
 
 
@@ -339,6 +374,16 @@
         copy.wait()
 
 
+def merged(picks):
+    joined = []
+    for place, low, high in picks:
+        if joined and joined[-1][0] == place and joined[-1][2] == low:
+            joined[-1] = (place, joined[-1][1], high)
+        else:
+            joined.append((place, low, high))
+    return joined
+
+
 def plan_of(chips):
     half = chips // 2
     far = list(range(half, chips))
@@ -347,8 +392,10 @@
     for i, bit in enumerate(far):
         send += [bit] if i == len(far) - 1 else [bit] + near[i : i + 1]
     early = far[: len(far) // 2]
-    stages = [[0, early[0], near[0]], early[1:] + near[1:], far[len(early) : -1], far[-1:]]
-    return send, stages, far[len(early) :] + early + near
+    stages = [[0, near[0], early[0]], near[1:] + early[1:], far[len(early) : -1], far[-1:]]
+    alike = [bit for bit in near if bit < half // 2]
+    other = [bit for bit in near if bit >= half // 2]
+    return send, stages, far[len(early) : -1] + early + far[-1:] + alike + other[::-1]
 
 
 def by_heads(q_rows, k_rows, v_rows, block_of, modality, out_gain):
@@ -360,38 +407,56 @@
     def across(x, bit):
         return lax.ppermute(x, "seq", [(i, i ^ (CORES * bit)) for i in range(peers)])
 
-    sent = list(pack(send[:FIRST], *rows_in))
-    *more, own = pack(send[FIRST:] + [0], *rows_in)
+    last = send[-1]
+    jobs = [(bit, "qkv") for bit in send[:-1]] + [(last, "kv"), (last, "q")]
+    sent = list(pack(jobs[:FIRST], *rows_in))
+    *more, own = pack(jobs[FIRST:] + [(0, "qkv")], *rows_in)
     direct, passed = {0: own}, {}
-    for bit, chunk in zip(send, sent + more):
-        direct[bit] = across(chunk, bit)
+    for (bit, parts), chunk in zip(jobs, sent + more):
+        chunk = across(chunk, bit)
+        if parts == "q":
+            query = chunk
+        else:
+            direct[bit] = chunk
     for bit in [bit for bits in stages for bit in bits]:
         passed[bit] = lax.ppermute(direct[bit], "seq", [(i, i ^ 1) for i in range(peers)])
     gain = pltpu.with_memory_space_constraint(out_gain, pltpu.HBM)
     sets, taken = [], []
-    for number, bits in enumerate(stages):
-        last = number == len(stages) - 1
+    for bits in stages[:-1]:
         chunks = [direct[bit] for bit in bits] + [passed[bit] for bit in bits]
-        operands = [x for one in sets for x in one] + chunks
         pairs = len(bits) * (2 * sum(len(one) for one in taken) + len(bits))
         laid = laid_shapes(len(bits), rows)
-        if last:
-            counts = [len(one) for one in taken]
-            kernel = functools.partial(out_kernel, counts, bits)
-            shapes = [((rows, CORES * HEAD_DIM), q_rows.dtype)] * (sum(counts) + len(bits))
-            done = call(kernel, gain, operands, shapes, laid, pairs, rows)
-        else:
-            kernel = functools.partial(stage_kernel, len(sets), bits)
-            shapes = [(one[0].shape, jnp.float32) for one in sets]
-            shapes += [((CORES, len(bits) * rows, HEAD_DIM), jnp.float32)] + laid
-            made = call(kernel, gain, operands, shapes, [], pairs, rows, not sets)
-            if not sets:
-                gain = made.pop()
-            old = len(sets)
-            sets = [[total] + one[1:] for total, one in zip(made, sets)] + [made[old:]]
+        shapes = [(one[0].shape, jnp.float32) for one in sets]
+        shapes += [((CORES, len(bits) * rows, HEAD_DIM), jnp.float32)] + laid
+        kernel = functools.partial(stage_kernel, len(sets), bits)
+        operands = [x for one in sets for x in one] + chunks
+        made = call(kernel, gain, operands, shapes, [], pairs, rows, not sets)
+        if not sets:
+            gain = made.pop()
+        old = len(sets)
+        sets = [[total] + one[1:] for total, one in zip(made, sets)] + [made[old:]]
         taken.append(bits)
-    owners = [bit for bits in taken for bit in bits]
-    done = dict(zip(owners, done))
+    flat = [x for one in sets for x in one]
+    piece = ((rows, CORES * HEAD_DIM), q_rows.dtype)
+    half = peers // CORES // 2
+    picks, owners = {True: [], False: []}, {True: [], False: []}
+    for place, bits in enumerate(taken):
+        for low, bit in enumerate(bits):
+            picks[bit >= half].append((place, low, low + 1))
+            owners[bit >= half].append(bit)
+    kernel = functools.partial(rest_kernel, merged(picks[True]), len(sets), [last])
+    shapes = [piece] * len(owners[True]) + laid_shapes(1, rows)
+    operands = flat + [direct[last], passed[last]]
+    made = call(kernel, gain, operands, shapes, [], len(owners[True]), rows)
+    count = len(owners[True])
+    done, laid = dict(zip(owners[True], made)), made[count:]
+    kernel = functools.partial(new_kernel, len(sets))
+    done[last] = call(kernel, query, laid + flat, [piece], [], peers // CORES, rows)[0]
+    kernel = functools.partial(rest_kernel, merged(picks[False]), len(sets), [])
+    shapes = [piece] * len(owners[False])
+    made = call(kernel, gain, flat + laid, shapes, [], len(owners[False]), rows)
+    done.update(zip(owners[False], made))
+    owners = list(done)
     for bit in order:
         done[bit] = across(done[bit], bit)
     back = [done[bit] for bit in owners]

time: 70 us -> 73.1 us (1.044)
  starting transfers between devices: 30.6 us -> 38.5 us
  waiting for transfers between devices: 27.7 us -> 21.9 us
  Pallas kernels: 11.4 us -> 12.3 us
    ppermute x14 -> x15, starting transfers between devices: 28.9 us -> 36.8 us  [across(): return lax.ppermute(x, 'seq', [(i, i ^ CORES * bit) for i in range(peers)])]
    ppermute x14 -> x15, waiting for transfers between devices: 27.6 us -> 21.9 us  [across(): return lax.ppermute(x, 'seq', [(i, i ^ CORES * bit) for i in range(peers)])]
    pallas_call x4 -> x6, Pallas kernels: 7.99 us -> 8.86 us  [call(): pl.pallas_call(kernel, in_specs=[HBM if read else VMEM] + [VMEM] * len(op...]
  transfers between devices with their start and end apart: 22 -> 23, of which waited for: 9 -> 5; matrix products, arithmetic and copies ran while one was open for 0% -> 0% of each run, Pallas kernels for 10% -> 14%
where the time goes in v4:
time: 73.1 us; the launch traced here: 72.8 us
  starting transfers between devices  38.5 us (53%)
  waiting for transfers between devices  21.9 us (30%)
  Pallas kernels  12.3 us (17%)
    ppermute x15, starting transfers between devices, across(): return lax.ppermute(x, 'seq', [(i, i ^ CORES * bit) for i in range(peers)])  36.8 us
    ppermute x15, waiting for transfers between devices, across(): return lax.ppermute(x, 'seq', [(i, i ^ CORES * bit) for i in range(peers)])  21.9 us
    pallas_call x6, Pallas kernels, call(): pl.pallas_call(kernel, in_specs=[HBM if read else VMEM] + [VMEM] * len(op...  8.86 us
    pallas_call x2, Pallas kernels, pack(): pl.pallas_call(functools.partial(pack_kernel, jobs), in_specs=[HBM] * len...  2.6 us
    ppermute x8, starting transfers between devices, by_heads(): lax.ppermute(direct[bit], 'seq', [(i, i ^ 1) for i in range(peers)])  1.65 us
  transfers between devices with their start and end apart: 23, of which 5 were waited for; matrix products, arithmetic and copies ran while one was open for 0% of the time, Pallas kernels for 14%

profile of v4, /device:TPU:0, one launch (start us, length us, event | category | flops | bytes accessed | tf_op | source)
XLA Modules:
  0.0 72.8 jit_solution(567787860690718835)
XLA Ops:
  0.0 1.5 %shard_map.64 = (bf16[392,256]{1,0:T(8,128)(2,1)S(1)}, bf16[392,256]{1,0:T(8,128)(2,1)S(1)}, bf16[392,256]{1,0:T(8,128)(2,1)S(1)}, bf16[392,256]{1,0:T(8,128)(2,...) custom-call(bf16[128,2048]{1,0:T(8,128)(2,1)} %q_ref.3, ...), custom_call_target="tpu_custom_call" | custom-call | flops 1048576 | bytes 1835008 | tf_op jit(solution)/shard_map/pallas_call | solution.py:155
  2.1 1.1 %shard_map.65 = (bf16[392,256]{1,0:T(8,128)(2,1)S(1)}, bf16[392,256]{1,0:T(8,128)(2,1)S(1)}) custom-call(bf16[128,2048]{1,0:T(8,128)(2,1)} %q_ref.3, bf16[128,2048]{1,0:T(8,128)(2,1)} %k_ref.3, bf16[128,2048]{1,0:T(8,128)(2,1)} %v_ref.3, s32[1,128]{1,0:T(1,128)} %bitcast.3, s32[1,128]{1,0:T(1,128)} %bitcast.5), custom_call_target="tpu_custom_call" | custom-call | flops 1048576 | bytes 524288 | tf_op jit(solution)/shard_map/pallas_call | solution.py:155
  3.2 2.6 %collective-permute-start = (bf16[392,256]{1,0:T(8,128)(2,1)S(1)}, bf16[392,256]{1,0:T(8,128)(2,1)S(1)}, u32[]{:S(2)}, u32[]{:S(2)}) collective-permute-start(bf16[392,256]{1,0:T(8,128)(2,1)S(1)} %get-tuple-element.53), channel_id=1, source_target_pairs={{0,4},{1,5},{2,6},{3,7},{4,0},{5,1},{6,2},{7,3},{8,12},{9,13},{10,... | collective-permute-start | bytes 602120 | tf_op jit(solution)/shard_map/ppermute | solution.py:408
  5.8 3.4 %collective-permute-start.13 = (bf16[264,256]{1,0:T(8,128)(2,1)S(1)}, bf16[264,256]{1,0:T(8,128)(2,1)S(1)}, u32[]{:S(2)}, u32[]{:S(2)}) collective-permute-start(bf16[264,256]{1,0:T(8,128)(2,1)S(1)} %get-tuple-element.84), channel_id=1, source_target_pairs={{0,14},{1,15},{2,12},{3,13},{4,10},{5,11},{6,8},{7,9},{8,6},{9,7},... | collective-permute-start | bytes 405512 | tf_op jit(solution)/shard_map/ppermute | solution.py:408
  9.3 2.9 %collective-permute-start.7 = (bf16[392,256]{1,0:T(8,128)(2,1)S(1)}, bf16[392,256]{1,0:T(8,128)(2,1)S(1)}, u32[]{:S(2)}, u32[]{:S(2)}) collective-permute-start(bf16[392,256]{1,0:T(8,128)(2,1)S(1)} %get-tuple-element.65), channel_id=1, source_target_pairs={{0,10},{1,11},{2,8},{3,9},{4,14},{5,15},{6,12},{7,13},{8,2},{9,3},... | collective-permute-start | bytes 602120 | tf_op jit(solution)/shard_map/ppermute | solution.py:408
  12.1 6.0 %collective-permute-done.13.refs_21_ = bf16[264,256]{1,0:T(8,128)(2,1)S(1)} collective-permute-done((bf16[264,256]{1,0:T(8,128)(2,1)S(1)}, bf16[264,256]{1,0:T(8,128)(2,1)S(1)}, u32[]{:S(2)}, u32[]{:S(2)}) %collective-permute-start.13) | collective-permute-done | bytes 135200 | tf_op jit(solution)/shard_map/ppermute | solution.py:408
  18.1 6.9 %collective-permute-start.5 = (bf16[392,256]{1,0:T(8,128)(2,1)S(1)}, bf16[392,256]{1,0:T(8,128)(2,1)S(1)}, u32[]{:S(2)}, u32[]{:S(2)}) collective-permute-start(bf16[392,256]{1,0:T(8,128)(2,1)S(1)} %get-tuple-element.63), channel_id=1, source_target_pairs={{0,6},{1,7},{2,4},{3,5},{4,2},{5,3},{6,0},{7,1},{8,14},{9,15},{10,... | collective-permute-start | bytes 602120 | tf_op jit(solution)/shard_map/ppermute | solution.py:408
  25.0 1.8 %collective-permute-start.6 = (bf16[392,256]{1,0:T(8,128)(2,1)S(1)}, bf16[392,256]{1,0:T(8,128)(2,1)S(1)}, u32[]{:S(2)}, u32[]{:S(2)}) collective-permute-start(bf16[392,256]{1,0:T(8,128)(2,1)S(1)} %get-tuple-element.64), channel_id=1, source_target_pairs={{0,2},{1,3},{2,0},{3,1},{4,6},{5,7},{6,4},{7,5},{8,10},{9,11},{10,... | collective-permute-start | bytes 602120 | tf_op jit(solution)/shard_map/ppermute | solution.py:408
  26.9 3.5 %collective-permute-start.11 = (bf16[392,256]{1,0:T(8,128)(2,1)S(1)}, bf16[392,256]{1,0:T(8,128)(2,1)S(1)}, u32[]{:S(2)}, u32[]{:S(2)}) collective-permute-start(bf16[392,256]{1,0:T(8,128)(2,1)S(1)} %get-tuple-element.74), channel_id=1, source_target_pairs={{0,12},{1,13},{2,14},{3,15},{4,8},{5,9},{6,10},{7,11},{8,4},{9,5},... | collective-permute-start | bytes 602120 | tf_op jit(solution)/shard_map/ppermute | solution.py:408
  30.4 7.8 %collective-permute-done.7.refs_9_ = bf16[392,256]{1,0:T(8,128)(2,1)S(1)} collective-permute-done((bf16[392,256]{1,0:T(8,128)(2,1)S(1)}, bf16[392,256]{1,0:T(8,128)(2,1)S(1)}, u32[]{:S(2)}, u32[]{:S(2)}) %collective-permute-start.7) | collective-permute-done | bytes 200736 | tf_op jit(solution)/shard_map/ppermute | solution.py:408
  38.3 1.6 %collective-permute-done.5.refs_7_ = bf16[392,256]{1,0:T(8,128)(2,1)S(1)} collective-permute-done((bf16[392,256]{1,0:T(8,128)(2,1)S(1)}, bf16[392,256]{1,0:T(8,128)(2,1)S(1)}, u32[]{:S(2)}, u32[]{:S(2)}) %collective-permute-start.5) | collective-permute-done | bytes 200736 | tf_op jit(solution)/shard_map/ppermute | solution.py:408
  40.9 1.8 %shard_map.66 = (f32[2,384,128]{2,1,0:T(8,128)S(1)}, bf16[2,384,128]{2,1,0:T(8,128)(2,1)S(1)}, bf16[2,768,128]{2,1,0:T(8,128)(2,1)S(1)}, bf16[2,768,128]{2,1,0:T...) custom-call(f32[3,2048]{1,0:T(4,128)} %gain_ref.1, ...), custom_call_target="tpu_custom_call" | custom-call | flops 301989888 | bytes 1048576 | tf_op jit(solution)/shard_map/pallas_call | solution.py:347
  42.8 3.7 %collective-permute-start.18 = (bf16[128,256]{1,0:T(8,128)(2,1)S(1)}, bf16[128,256]{1,0:T(8,128)(2,1)S(1)}, u32[]{:S(2)}, u32[]{:S(2)}) collective-permute-start(bf16[128,256]{1,0:T(8,128)(2,1)S(1)} %get-tuple-element.88), channel_id=1, source_target_pairs={{0,14},{1,15},{2,12},{3,13},{4,10},{5,11},{6,8},{7,9},{8,6},{9,7},... | collective-permute-start | bytes 196616 | tf_op jit(solution)/shard_map/ppermute | solution.py:408
  46.5 2.6 %shard_map.67 = (f32[2,384,128]{2,1,0:T(8,128)S(1)}, f32[2,384,128]{2,1,0:T(8,128)S(1)}, bf16[2,384,128]{2,1,0:T(8,128)(2,1)S(1)}, bf16[2,768,128]{2,1,0:T(8,128...) custom-call(f32[3,256]{1,0:T(4,128)S(1)} %get-tuple-element.55.gain_, ...), custom_call_target="tpu_custom_call" | custom-call | flops 905969664 | bytes 1048576 | tf_op jit(solution)/shard_map/pallas_call | solution.py:347
  49.1 1.7 %shard_map.68 = (f32[2,384,128]{2,1,0:T(8,128)S(1)}, f32[2,384,128]{2,1,0:T(8,128)S(1)}, f32[2,128,128]{2,1,0:T(8,128)S(1)}, bf16[2,128,128]{2,1,0:T(8,128)(2,1)...) custom-call(f32[3,256]{1,0:T(4,128)S(1)} %get-tuple-element.55.gain_, ...), custom_call_target="tpu_custom_call" | custom-call | flops 436207616 | bytes 1048576 | tf_op jit(solution)/shard_map/pallas_call | solution.py:347
  51.5 0.8 %shard_map.71 = (bf16[128,256]{1,0:T(8,128)(2,1)S(1)}, bf16[128,256]{1,0:T(8,128)(2,1)S(1)}, bf16[128,256]{1,0:T(8,128)(2,1)S(1)}, bf16[128,256]{1,0:T(8,128)(2,1)S(1)}) custom-call(f32[3,256]{1,0:T(4,128)S(1)} %get-tuple-element.55.gain_ref, f32[2,384,128]{2,1,0:T(8,128)S(1)} %get-tuple-element.75.refs_0_.refs_6_, ...), custom_call_target="tpu_custom_call" | custom-call | flops 134217728 | bytes 1048576 | tf_op jit(solution)/shard_map/pallas_call | solution.py:347
  52.7 3.7 %collective-permute-start.21 = (bf16[128,256]{1,0:T(8,128)(2,1)S(1)}, bf16[128,256]{1,0:T(8,128)(2,1)S(1)}, u32[]{:S(2)}, u32[]{:S(2)}) collective-permute-start(bf16[128,256]{1,0:T(8,128)(2,1)S(1)} %get-tuple-element.97), channel_id=1, source_target_pairs={{0,6},{1,7},{2,4},{3,5},{4,2},{5,3},{6,0},{7,1},{8,14},{9,15},{10,... | collective-permute-start | bytes 196616 | tf_op jit(solution)/shard_map/ppermute | solution.py:408
  56.5 1.2 %shard_map.70 = bf16[128,256]{1,0:T(8,128)(2,1)S(1)} custom-call(bf16[128,256]{1,0:T(8,128)(2,1)S(1)} %collective-permute-done.18.query_ref, bf16[2,128,128]{2,1,0:T(8,128)(2,1)S(1)} %get-tuple-element.89.refs_0_.refs_21_, bf16[2,256,128]{2,1,0:T(8,128)(2,1)S(1)} %get-tuple-element.90.refs_1_.refs_22_, ...), custom_call_target="tpu_custom_call" | custom-call | flops 268435456 | bytes 1048576 | tf_op jit(solution)/shard_map/pallas_call | solution.py:347
  58.3 2.5 %collective-permute-start.15 = (bf16[128,256]{1,0:T(8,128)(2,1)S(1)}, bf16[128,256]{1,0:T(8,128)(2,1)S(1)}, u32[]{:S(2)}, u32[]{:S(2)}) collective-permute-start(bf16[128,256]{1,0:T(8,128)(2,1)S(1)} %get-tuple-element.85), channel_id=1, source_target_pairs={{0,8},{1,9},{2,10},{3,11},{4,12},{5,13},{6,14},{7,15},{8,0},{9,1},... | collective-permute-start | bytes 196616 | tf_op jit(solution)/shard_map/ppermute | solution.py:408
  60.8 1.5 %collective-permute-start.16 = (bf16[128,256]{1,0:T(8,128)(2,1)S(1)}, bf16[128,256]{1,0:T(8,128)(2,1)S(1)}, u32[]{:S(2)}, u32[]{:S(2)}) collective-permute-start(bf16[128,256]{1,0:T(8,128)(2,1)S(1)} %get-tuple-element.86), channel_id=1, source_target_pairs={{0,10},{1,11},{2,8},{3,9},{4,14},{5,15},{6,12},{7,13},{8,2},{9,3},... | collective-permute-start | bytes 196616 | tf_op jit(solution)/shard_map/ppermute | solution.py:408
  62.2 3.2 %collective-permute-start.17 = (bf16[128,256]{1,0:T(8,128)(2,1)S(1)}, bf16[128,256]{1,0:T(8,128)(2,1)S(1)}, u32[]{:S(2)}, u32[]{:S(2)}) collective-permute-start(bf16[128,256]{1,0:T(8,128)(2,1)S(1)} %get-tuple-element.87), channel_id=1, source_target_pairs={{0,12},{1,13},{2,14},{3,15},{4,8},{5,9},{6,10},{7,11},{8,4},{9,5},... | collective-permute-start | bytes 196616 | tf_op jit(solution)/shard_map/ppermute | solution.py:408
  65.4 4.6 %collective-permute-done.15.refs_0_ = bf16[128,256]{1,0:T(8,128)(2,1)S(1)} collective-permute-done((bf16[128,256]{1,0:T(8,128)(2,1)S(1)}, bf16[128,256]{1,0:T(8,128)(2,1)S(1)}, u32[]{:S(2)}, u32[]{:S(2)}) %collective-permute-start.15) | collective-permute-done | bytes 65568 | tf_op jit(solution)/shard_map/ppermute | solution.py:408
  70.1 1.9 %collective-permute-done.16.refs_1_ = bf16[128,256]{1,0:T(8,128)(2,1)S(1)} collective-permute-done((bf16[128,256]{1,0:T(8,128)(2,1)S(1)}, bf16[128,256]{1,0:T(8,128)(2,1)S(1)}, u32[]{:S(2)}, u32[]{:S(2)}) %collective-permute-start.16) | collective-permute-done | bytes 65568 | tf_op jit(solution)/shard_map/ppermute | solution.py:408
  72.0 0.8 %shard_map.72 = bf16[128,2048]{1,0:T(8,128)(2,1)} custom-call(bf16[128,256]{1,0:T(8,128)(2,1)S(1)} %collective-permute-done.15.refs_0_, bf16[128,256]{1,0:T(8,128)(2,1)S(1)} %collective-permute-done.16.refs_1_, bf16[128,256]{1,0:T(8,128)(2,1)S(1)} %collective-permute-done.17.refs_2_, bf16[128,256]{1,0:T(8,128)(2,1)S(1)} %collective-permute-done.19.refs_3_, ...), custom_call_target="tpu_custom_call" | custom-call | tf_op jit(solution)/shard_map/pallas_call | solution.py:463
  (31 shorter events, 3.5 us)
Async XLA Ops:
  1.5 23.5 %collective-permute-start.2 = (bf16[392,256]{1,0:T(8,128)(2,1)S(1)}, bf16[392,256]{1,0:T(8,128)(2,1)S(1)}, u32[]{:S(2)}, u32[]{:S(2)}) collective-permute-start(bf16[392,256]{1,0:T(8,128)(2,1)S(1)} %get-tuple-element.52.refs_0_), channel_id=1, source_target_pairs={{0,1},{1,0},{2,3},{3,2},{4,5},{5,4},{6,7},{7,6},{8,9},{9,8},{10,11... | collective-permute-start | bytes 602120 | tf_op jit(solution)/shard_map/ppermute | solution.py:422
  3.2 23.7 %collective-permute-start = (bf16[392,256]{1,0:T(8,128)(2,1)S(1)}, bf16[392,256]{1,0:T(8,128)(2,1)S(1)}, u32[]{:S(2)}, u32[]{:S(2)}) collective-permute-start(bf16[392,256]{1,0:T(8,128)(2,1)S(1)} %get-tuple-element.53), channel_id=1, source_target_pairs={{0,4},{1,5},{2,6},{3,7},{4,0},{5,1},{6,2},{7,3},{8,12},{9,13},{10,... | collective-permute-start | bytes 602120 | tf_op jit(solution)/shard_map/ppermute | solution.py:408
  5.8 12.3 %collective-permute-start.13 = (bf16[264,256]{1,0:T(8,128)(2,1)S(1)}, bf16[264,256]{1,0:T(8,128)(2,1)S(1)}, u32[]{:S(2)}, u32[]{:S(2)}) collective-permute-start(bf16[264,256]{1,0:T(8,128)(2,1)S(1)} %get-tuple-element.84), channel_id=1, source_target_pairs={{0,14},{1,15},{2,12},{3,13},{4,10},{5,11},{6,8},{7,9},{8,6},{9,7},... | collective-permute-start | bytes 405512 | tf_op jit(solution)/shard_map/ppermute | solution.py:408
  9.2 21.2 %collective-permute-start.1 = (bf16[392,256]{1,0:T(8,128)(2,1)S(1)}, bf16[392,256]{1,0:T(8,128)(2,1)S(1)}, u32[]{:S(2)}, u32[]{:S(2)}) collective-permute-start(bf16[392,256]{1,0:T(8,128)(2,1)S(1)} %get-tuple-element.54), channel_id=1, source_target_pairs={{0,8},{1,9},{2,10},{3,11},{4,12},{5,13},{6,14},{7,15},{8,0},{9,1},... | collective-permute-start | bytes 602120 | tf_op jit(solution)/shard_map/ppermute | solution.py:408
  9.3 29.0 %collective-permute-start.7 = (bf16[392,256]{1,0:T(8,128)(2,1)S(1)}, bf16[392,256]{1,0:T(8,128)(2,1)S(1)}, u32[]{:S(2)}, u32[]{:S(2)}) collective-permute-start(bf16[392,256]{1,0:T(8,128)(2,1)S(1)} %get-tuple-element.65), channel_id=1, source_target_pairs={{0,10},{1,11},{2,8},{3,9},{4,14},{5,15},{6,12},{7,13},{8,2},{9,3},... | collective-permute-start | bytes 602120 | tf_op jit(solution)/shard_map/ppermute | solution.py:408
  18.1 21.7 %collective-permute-start.5 = (bf16[392,256]{1,0:T(8,128)(2,1)S(1)}, bf16[392,256]{1,0:T(8,128)(2,1)S(1)}, u32[]{:S(2)}, u32[]{:S(2)}) collective-permute-start(bf16[392,256]{1,0:T(8,128)(2,1)S(1)} %get-tuple-element.63), channel_id=1, source_target_pairs={{0,6},{1,7},{2,4},{3,5},{4,2},{5,3},{6,0},{7,1},{8,14},{9,15},{10,... | collective-permute-start | bytes 602120 | tf_op jit(solution)/shard_map/ppermute | solution.py:408
  25.0 14.8 %collective-permute-start.6 = (bf16[392,256]{1,0:T(8,128)(2,1)S(1)}, bf16[392,256]{1,0:T(8,128)(2,1)S(1)}, u32[]{:S(2)}, u32[]{:S(2)}) collective-permute-start(bf16[392,256]{1,0:T(8,128)(2,1)S(1)} %get-tuple-element.64), channel_id=1, source_target_pairs={{0,2},{1,3},{2,0},{3,1},{4,6},{5,7},{6,4},{7,5},{8,10},{9,11},{10,... | collective-permute-start | bytes 602120 | tf_op jit(solution)/shard_map/ppermute | solution.py:408
  26.9 13.5 %collective-permute-start.11 = (bf16[392,256]{1,0:T(8,128)(2,1)S(1)}, bf16[392,256]{1,0:T(8,128)(2,1)S(1)}, u32[]{:S(2)}, u32[]{:S(2)}) collective-permute-start(bf16[392,256]{1,0:T(8,128)(2,1)S(1)} %get-tuple-element.74), channel_id=1, source_target_pairs={{0,12},{1,13},{2,14},{3,15},{4,8},{5,9},{6,10},{7,11},{8,4},{9,5},... | collective-permute-start | bytes 602120 | tf_op jit(solution)/shard_map/ppermute | solution.py:408
  30.4 10.0 %collective-permute-start.3 = (bf16[392,256]{1,0:T(8,128)(2,1)S(1)}, bf16[392,256]{1,0:T(8,128)(2,1)S(1)}, u32[]{:S(2)}, u32[]{:S(2)}) collective-permute-start(bf16[392,256]{1,0:T(8,128)(2,1)S(1)} %collective-permute-done.refs_1_), channel_id=1, source_target_pairs={{0,1},{1,0},{2,3},{3,2},{4,5},{5,4},{6,7},{7,6},{8,9},{9,8},{10,11... | collective-permute-start | bytes 602120 | tf_op jit(solution)/shard_map/ppermute | solution.py:422
  38.2 2.6 %collective-permute-start.4 = (bf16[392,256]{1,0:T(8,128)(2,1)S(1)}, bf16[392,256]{1,0:T(8,128)(2,1)S(1)}, u32[]{:S(2)}, u32[]{:S(2)}) collective-permute-start(bf16[392,256]{1,0:T(8,128)(2,1)S(1)} %collective-permute-done.1.refs_2_), channel_id=1, source_target_pairs={{0,1},{1,0},{2,3},{3,2},{4,5},{5,4},{6,7},{7,6},{8,9},{9,8},{10,11... | collective-permute-start | bytes 602120 | tf_op jit(solution)/shard_map/ppermute | solution.py:422
  39.8 3.0 %collective-permute-start.10 = (bf16[392,256]{1,0:T(8,128)(2,1)S(1)}, bf16[392,256]{1,0:T(8,128)(2,1)S(1)}, u32[]{:S(2)}, u32[]{:S(2)}) collective-permute-start(bf16[392,256]{1,0:T(8,128)(2,1)S(1)} %collective-permute-done.7.refs_9_), channel_id=1, source_target_pairs={{0,1},{1,0},{2,3},{3,2},{4,5},{5,4},{6,7},{7,6},{8,9},{9,8},{10,11... | collective-permute-start | bytes 602120 | tf_op jit(solution)/shard_map/ppermute | solution.py:422
  39.8 6.6 %collective-permute-start.8 = (bf16[392,256]{1,0:T(8,128)(2,1)S(1)}, bf16[392,256]{1,0:T(8,128)(2,1)S(1)}, u32[]{:S(2)}, u32[]{:S(2)}) collective-permute-start(bf16[392,256]{1,0:T(8,128)(2,1)S(1)} %collective-permute-done.5.refs_7_), channel_id=1, source_target_pairs={{0,1},{1,0},{2,3},{3,2},{4,5},{5,4},{6,7},{7,6},{8,9},{9,8},{10,11... | collective-permute-start | bytes 602120 | tf_op jit(solution)/shard_map/ppermute | solution.py:422
  40.3 6.1 %collective-permute-start.9 = (bf16[392,256]{1,0:T(8,128)(2,1)S(1)}, bf16[392,256]{1,0:T(8,128)(2,1)S(1)}, u32[]{:S(2)}, u32[]{:S(2)}) collective-permute-start(bf16[392,256]{1,0:T(8,128)(2,1)S(1)} %collective-permute-done.6.refs_8_), channel_id=1, source_target_pairs={{0,1},{1,0},{2,3},{3,2},{4,5},{5,4},{6,7},{7,6},{8,9},{9,8},{10,11... | collective-permute-start | bytes 602120 | tf_op jit(solution)/shard_map/ppermute | solution.py:422
  40.4 8.7 %collective-permute-start.12 = (bf16[392,256]{1,0:T(8,128)(2,1)S(1)}, bf16[392,256]{1,0:T(8,128)(2,1)S(1)}, u32[]{:S(2)}, u32[]{:S(2)}) collective-permute-start(bf16[392,256]{1,0:T(8,128)(2,1)S(1)} %collective-permute-done.11.refs_14_), channel_id=1, source_target_pairs={{0,1},{1,0},{2,3},{3,2},{4,5},{5,4},{6,7},{7,6},{8,9},{9,8},{10,11... | collective-permute-start | bytes 602120 | tf_op jit(solution)/shard_map/ppermute | solution.py:422
  40.9 9.9 %collective-permute-start.14 = (bf16[264,256]{1,0:T(8,128)(2,1)S(1)}, bf16[264,256]{1,0:T(8,128)(2,1)S(1)}, u32[]{:S(2)}, u32[]{:S(2)}) collective-permute-start(bf16[264,256]{1,0:T(8,128)(2,1)S(1)} %collective-permute-done.13.refs_21_), channel_id=1, source_target_pairs={{0,1},{1,0},{2,3},{3,2},{4,5},{5,4},{6,7},{7,6},{8,9},{9,8},{10,11... | collective-permute-start | bytes 405512 | tf_op jit(solution)/shard_map/ppermute | solution.py:422
  42.8 13.7 %collective-permute-start.18 = (bf16[128,256]{1,0:T(8,128)(2,1)S(1)}, bf16[128,256]{1,0:T(8,128)(2,1)S(1)}, u32[]{:S(2)}, u32[]{:S(2)}) collective-permute-start(bf16[128,256]{1,0:T(8,128)(2,1)S(1)} %get-tuple-element.88), channel_id=1, source_target_pairs={{0,14},{1,15},{2,12},{3,13},{4,10},{5,11},{6,8},{7,9},{8,6},{9,7},... | collective-permute-start | bytes 196616 | tf_op jit(solution)/shard_map/ppermute | solution.py:408
  52.3 8.5 %collective-permute-start.20 = (bf16[128,256]{1,0:T(8,128)(2,1)S(1)}, bf16[128,256]{1,0:T(8,128)(2,1)S(1)}, u32[]{:S(2)}, u32[]{:S(2)}) collective-permute-start(bf16[128,256]{1,0:T(8,128)(2,1)S(1)} %get-tuple-element.96), channel_id=1, source_target_pairs={{0,4},{1,5},{2,6},{3,7},{4,0},{5,1},{6,2},{7,3},{8,12},{9,13},{10,... | collective-permute-start | bytes 196616 | tf_op jit(solution)/shard_map/ppermute | solution.py:408
  52.7 9.5 %collective-permute-start.21 = (bf16[128,256]{1,0:T(8,128)(2,1)S(1)}, bf16[128,256]{1,0:T(8,128)(2,1)S(1)}, u32[]{:S(2)}, u32[]{:S(2)}) collective-permute-start(bf16[128,256]{1,0:T(8,128)(2,1)S(1)} %get-tuple-element.97), channel_id=1, source_target_pairs={{0,6},{1,7},{2,4},{3,5},{4,2},{5,3},{6,0},{7,1},{8,14},{9,15},{10,... | collective-permute-start | bytes 196616 | tf_op jit(solution)/shard_map/ppermute | solution.py:408
  56.5 9.0 %collective-permute-start.22 = (bf16[128,256]{1,0:T(8,128)(2,1)S(1)}, bf16[128,256]{1,0:T(8,128)(2,1)S(1)}, u32[]{:S(2)}, u32[]{:S(2)}) collective-permute-start(bf16[128,256]{1,0:T(8,128)(2,1)S(1)} %get-tuple-element.98), channel_id=1, source_target_pairs={{0,2},{1,3},{2,0},{3,1},{4,6},{5,7},{6,4},{7,5},{8,10},{9,11},{10,... | collective-permute-start | bytes 196616 | tf_op jit(solution)/shard_map/ppermute | solution.py:408
  57.7 7.7 %collective-permute-start.19 = (bf16[128,256]{1,0:T(8,128)(2,1)S(1)}, bf16[128,256]{1,0:T(8,128)(2,1)S(1)}, u32[]{:S(2)}, u32[]{:S(2)}) collective-permute-start(bf16[128,256]{1,0:T(8,128)(2,1)S(1)} %shard_map.70), channel_id=1, source_target_pairs={{0,14},{1,15},{2,12},{3,13},{4,10},{5,11},{6,8},{7,9},{8,6},{9,7},... | collective-permute-start | bytes 196616 | tf_op jit(solution)/shard_map/ppermute | solution.py:408
  58.3 11.8 %collective-permute-start.15 = (bf16[128,256]{1,0:T(8,128)(2,1)S(1)}, bf16[128,256]{1,0:T(8,128)(2,1)S(1)}, u32[]{:S(2)}, u32[]{:S(2)}) collective-permute-start(bf16[128,256]{1,0:T(8,128)(2,1)S(1)} %get-tuple-element.85), channel_id=1, source_target_pairs={{0,8},{1,9},{2,10},{3,11},{4,12},{5,13},{6,14},{7,15},{8,0},{9,1},... | collective-permute-start | bytes 196616 | tf_op jit(solution)/shard_map/ppermute | solution.py:408
  60.8 11.2 %collective-permute-start.16 = (bf16[128,256]{1,0:T(8,128)(2,1)S(1)}, bf16[128,256]{1,0:T(8,128)(2,1)S(1)}, u32[]{:S(2)}, u32[]{:S(2)}) collective-permute-start(bf16[128,256]{1,0:T(8,128)(2,1)S(1)} %get-tuple-element.86), channel_id=1, source_target_pairs={{0,10},{1,11},{2,8},{3,9},{4,14},{5,15},{6,12},{7,13},{8,2},{9,3},... | collective-permute-start | bytes 196616 | tf_op jit(solution)/shard_map/ppermute | solution.py:408
  62.2 9.7 %collective-permute-start.17 = (bf16[128,256]{1,0:T(8,128)(2,1)S(1)}, bf16[128,256]{1,0:T(8,128)(2,1)S(1)}, u32[]{:S(2)}, u32[]{:S(2)}) collective-permute-start(bf16[128,256]{1,0:T(8,128)(2,1)S(1)} %get-tuple-element.87), channel_id=1, source_target_pairs={{0,12},{1,13},{2,14},{3,15},{4,8},{5,9},{6,10},{7,11},{8,4},{9,5},... | collective-permute-start | bytes 196616 | tf_op jit(solution)/shard_map/ppermute | solution.py:408

commit v5 on v4

--- a/solution.py
+++ b/solution.py
@@ -361,7 +361,7 @@
 
 
 def unpack_kernel(bits, *refs):
-    *in_refs, out_ref, sems = refs
+    in_refs, (*_, out_ref, sems) = refs[: len(bits)], refs[len(bits) :]
     chip = lax.axis_index("seq") // CORES
     copies = []
     for i, (bit, in_ref) in enumerate(zip(bits, in_refs)):
@@ -456,18 +456,23 @@
     shapes = [piece] * len(owners[False])
     made = call(kernel, gain, flat + laid, shapes, [], len(owners[False]), rows)
     done.update(zip(owners[False], made))
-    owners = list(done)
     for bit in order:
         done[bit] = across(done[bit], bit)
-    back = [done[bit] for bit in owners]
-    return pl.pallas_call(
-        functools.partial(unpack_kernel, owners),
-        in_specs=[VMEM] * len(back),
-        out_specs=HBM,
-        out_shape=jax.ShapeDtypeStruct(q_rows.shape, q_rows.dtype),
-        scratch_shapes=[pltpu.SemaphoreType.DMA((len(back),))],
-        compiler_params=pltpu.CompilerParams(vmem_limit_bytes=8 << 20),
-    )(*back)
+    late = order[-4:]
+    out = []
+    for bits in ([0] + [x for x in order if x not in late], late):
+        out = [
+            pl.pallas_call(
+                functools.partial(unpack_kernel, bits),
+                in_specs=[VMEM] * len(bits) + [HBM] * len(out),
+                out_specs=HBM,
+                out_shape=jax.ShapeDtypeStruct(q_rows.shape, q_rows.dtype),
+                scratch_shapes=[pltpu.SemaphoreType.DMA((len(bits),))],
+                input_output_aliases={len(bits): 0} if out else {},
+                compiler_params=pltpu.CompilerParams(vmem_limit_bytes=8 << 20),
+            )(*[done[bit] for bit in bits], *out)
+        ]
+    return out[0]
 
 
 def fits_heads(peers, rows):

time: 73.1 us -> 67.4 us (0.922)
  starting transfers between devices: 38.5 us -> 30.2 us
  waiting for transfers between devices: 21.9 us -> 24 us
    ppermute x15, starting transfers between devices: 36.8 us -> 28.6 us  [across(): return lax.ppermute(x, 'seq', [(i, i ^ CORES * bit) for i in range(peers)])]
    ppermute x15, waiting for transfers between devices: 21.9 us -> 23.9 us  [across(): return lax.ppermute(x, 'seq', [(i, i ^ CORES * bit) for i in range(peers)])]
    pallas_call x1 -> x2, Pallas kernels: 0.85 us -> 1.47 us  [by_heads(): pl.pallas_call(functools.partial(unpack_kernel, bits), in_specs=[VMEM] *...]
  transfers between devices with their start and end apart: 23 -> 23, of which waited for: 5 -> 3; matrix products, arithmetic and copies ran while one was open for 0% -> 0% of each run, Pallas kernels for 14% -> 16%
where the time goes in v5:
time: 67.4 us; the launch traced here: 67.2 us
  starting transfers between devices  30.2 us (45%)
  waiting for transfers between devices  24 us (36%)
  Pallas kernels  12.9 us (19%)
    ppermute x15, starting transfers between devices, across(): return lax.ppermute(x, 'seq', [(i, i ^ CORES * bit) for i in range(peers)])  28.6 us
    ppermute x15, waiting for transfers between devices, across(): return lax.ppermute(x, 'seq', [(i, i ^ CORES * bit) for i in range(peers)])  23.9 us
    pallas_call x6, Pallas kernels, call(): pl.pallas_call(kernel, in_specs=[HBM if read else VMEM] + [VMEM] * len(op...  8.83 us
    pallas_call x2, Pallas kernels, pack(): pl.pallas_call(functools.partial(pack_kernel, jobs), in_specs=[HBM] * len...  2.6 us
    ppermute x8, starting transfers between devices, by_heads(): lax.ppermute(direct[bit], 'seq', [(i, i ^ 1) for i in range(peers)])  1.6 us
    pallas_call x2, Pallas kernels, by_heads(): pl.pallas_call(functools.partial(unpack_kernel, bits), in_specs=[VMEM] *...  1.47 us
  transfers between devices with their start and end apart: 23, of which 3 were waited for; matrix products, arithmetic and copies ran while one was open for 0% of the time, Pallas kernels for 16%

profile of v5, /device:TPU:0, one launch (start us, length us, event | category | flops | bytes accessed | tf_op | source)
XLA Modules:
  0.0 67.2 jit_solution(11309113898629729435)
XLA Ops:
  0.0 1.1 %shard_map.65 = (bf16[392,256]{1,0:T(8,128)(2,1)S(1)}, bf16[392,256]{1,0:T(8,128)(2,1)S(1)}) custom-call(bf16[128,2048]{1,0:T(8,128)(2,1)} %q_ref.3, bf16[128,2048]{1,0:T(8,128)(2,1)} %k_ref.3, bf16[128,2048]{1,0:T(8,128)(2,1)} %v_ref.3, s32[1,128]{1,0:T(1,128)} %bitcast.2, s32[1,128]{1,0:T(1,128)} %bitcast.4), custom_call_target="tpu_custom_call" | custom-call | flops 1048576 | bytes 524288 | tf_op jit(solution)/shard_map/pallas_call | solution.py:155
  1.1 3.1 %collective-permute-start.1 = (bf16[392,256]{1,0:T(8,128)(2,1)S(1)}, bf16[392,256]{1,0:T(8,128)(2,1)S(1)}, u32[]{:S(2)}, u32[]{:S(2)}) collective-permute-start(bf16[392,256]{1,0:T(8,128)(2,1)S(1)} %get-tuple-element.54), channel_id=1, source_target_pairs={{0,4},{1,5},{2,6},{3,7},{4,0},{5,1},{6,2},{7,3},{8,12},{9,13},{10,... | collective-permute-start | bytes 602120 | tf_op jit(solution)/shard_map/ppermute | solution.py:408
  4.2 2.6 %collective-permute-start.2 = (bf16[392,256]{1,0:T(8,128)(2,1)S(1)}, bf16[392,256]{1,0:T(8,128)(2,1)S(1)}, u32[]{:S(2)}, u32[]{:S(2)}) collective-permute-start(bf16[392,256]{1,0:T(8,128)(2,1)S(1)} %get-tuple-element.55), channel_id=1, source_target_pairs={{0,8},{1,9},{2,10},{3,11},{4,12},{5,13},{6,14},{7,15},{8,0},{9,1},... | collective-permute-start | bytes 602120 | tf_op jit(solution)/shard_map/ppermute | solution.py:408
  6.8 1.5 %shard_map.64 = (bf16[392,256]{1,0:T(8,128)(2,1)S(1)}, bf16[392,256]{1,0:T(8,128)(2,1)S(1)}, bf16[392,256]{1,0:T(8,128)(2,1)S(1)}, bf16[392,256]{1,0:T(8,128)(2,...) custom-call(bf16[128,2048]{1,0:T(8,128)(2,1)} %q_ref.3, ...), custom_call_target="tpu_custom_call" | custom-call | flops 1048576 | bytes 1835008 | tf_op jit(solution)/shard_map/pallas_call | solution.py:155
  8.3 1.2 %collective-permute-start.14 = (bf16[264,256]{1,0:T(8,128)(2,1)S(1)}, bf16[264,256]{1,0:T(8,128)(2,1)S(1)}, u32[]{:S(2)}, u32[]{:S(2)}) collective-permute-start(bf16[264,256]{1,0:T(8,128)(2,1)S(1)} %get-tuple-element.85), channel_id=1, source_target_pairs={{0,14},{1,15},{2,12},{3,13},{4,10},{5,11},{6,8},{7,9},{8,6},{9,7},... | collective-permute-start | bytes 405512 | tf_op jit(solution)/shard_map/ppermute | solution.py:408
  10.2 10.6 %collective-permute-done.14.refs_21_ = bf16[264,256]{1,0:T(8,128)(2,1)S(1)} collective-permute-done((bf16[264,256]{1,0:T(8,128)(2,1)S(1)}, bf16[264,256]{1,0:T(8,128)(2,1)S(1)}, u32[]{:S(2)}, u32[]{:S(2)}) %collective-permute-start.14) | collective-permute-done | bytes 135200 | tf_op jit(solution)/shard_map/ppermute | solution.py:408
  21.3 6.4 %collective-permute-start.8 = (bf16[392,256]{1,0:T(8,128)(2,1)S(1)}, bf16[392,256]{1,0:T(8,128)(2,1)S(1)}, u32[]{:S(2)}, u32[]{:S(2)}) collective-permute-start(bf16[392,256]{1,0:T(8,128)(2,1)S(1)} %get-tuple-element.66), channel_id=1, source_target_pairs={{0,10},{1,11},{2,8},{3,9},{4,14},{5,15},{6,12},{7,13},{8,2},{9,3},... | collective-permute-start | bytes 602120 | tf_op jit(solution)/shard_map/ppermute | solution.py:408
  27.7 1.2 %collective-permute-start.12 = (bf16[392,256]{1,0:T(8,128)(2,1)S(1)}, bf16[392,256]{1,0:T(8,128)(2,1)S(1)}, u32[]{:S(2)}, u32[]{:S(2)}) collective-permute-start(bf16[392,256]{1,0:T(8,128)(2,1)S(1)} %get-tuple-element.75), channel_id=1, source_target_pairs={{0,12},{1,13},{2,14},{3,15},{4,8},{5,9},{6,10},{7,11},{8,4},{9,5},... | collective-permute-start | bytes 602120 | tf_op jit(solution)/shard_map/ppermute | solution.py:408
  29.5 10.9 %collective-permute-done.8.refs_9_ = bf16[392,256]{1,0:T(8,128)(2,1)S(1)} collective-permute-done((bf16[392,256]{1,0:T(8,128)(2,1)S(1)}, bf16[392,256]{1,0:T(8,128)(2,1)S(1)}, u32[]{:S(2)}, u32[]{:S(2)}) %collective-permute-start.8) | collective-permute-done | bytes 200736 | tf_op jit(solution)/shard_map/ppermute | solution.py:408
  41.5 1.8 %shard_map.66 = (f32[2,384,128]{2,1,0:T(8,128)S(1)}, bf16[2,384,128]{2,1,0:T(8,128)(2,1)S(1)}, bf16[2,768,128]{2,1,0:T(8,128)(2,1)S(1)}, bf16[2,768,128]{2,1,0:T...) custom-call(f32[3,2048]{1,0:T(4,128)} %gain_ref.1, ...), custom_call_target="tpu_custom_call" | custom-call | flops 301989888 | bytes 1048576 | tf_op jit(solution)/shard_map/pallas_call | solution.py:347
  43.3 2.4 %collective-permute-start = (bf16[128,256]{1,0:T(8,128)(2,1)S(1)}, bf16[128,256]{1,0:T(8,128)(2,1)S(1)}, u32[]{:S(2)}, u32[]{:S(2)}) collective-permute-start(bf16[128,256]{1,0:T(8,128)(2,1)S(1)} %get-tuple-element.52), channel_id=1, source_target_pairs={{0,14},{1,15},{2,12},{3,13},{4,10},{5,11},{6,8},{7,9},{8,6},{9,7},... | collective-permute-start | bytes 196616 | tf_op jit(solution)/shard_map/ppermute | solution.py:408
  45.7 2.6 %shard_map.67 = (f32[2,384,128]{2,1,0:T(8,128)S(1)}, f32[2,384,128]{2,1,0:T(8,128)S(1)}, bf16[2,384,128]{2,1,0:T(8,128)(2,1)S(1)}, bf16[2,768,128]{2,1,0:T(8,128...) custom-call(f32[3,256]{1,0:T(4,128)S(1)} %get-tuple-element.56.gain_, ...), custom_call_target="tpu_custom_call" | custom-call | flops 905969664 | bytes 1048576 | tf_op jit(solution)/shard_map/pallas_call | solution.py:347
  48.4 1.7 %shard_map.68 = (f32[2,384,128]{2,1,0:T(8,128)S(1)}, f32[2,384,128]{2,1,0:T(8,128)S(1)}, f32[2,128,128]{2,1,0:T(8,128)S(1)}, bf16[2,128,128]{2,1,0:T(8,128)(2,1)...) custom-call(f32[3,256]{1,0:T(4,128)S(1)} %get-tuple-element.56.gain_, ...), custom_call_target="tpu_custom_call" | custom-call | flops 436207616 | bytes 1048576 | tf_op jit(solution)/shard_map/pallas_call | solution.py:347
  50.0 0.8 %shard_map.69 = (bf16[128,256]{1,0:T(8,128)(2,1)S(1)}, bf16[128,256]{1,0:T(8,128)(2,1)S(1)}, bf16[128,256]{1,0:T(8,128)(2,1)S(1)}, bf16[2,128,128]{2,1,0:T(8,128...) custom-call(f32[3,256]{1,0:T(4,128)S(1)} %get-tuple-element.56.gain_, ...), custom_call_target="tpu_custom_call" | custom-call | flops 100663296 | bytes 1048576 | tf_op jit(solution)/shard_map/pallas_call | solution.py:347
  50.8 1.4 %collective-permute-start.20 = (bf16[128,256]{1,0:T(8,128)(2,1)S(1)}, bf16[128,256]{1,0:T(8,128)(2,1)S(1)}, u32[]{:S(2)}, u32[]{:S(2)}) collective-permute-start(bf16[128,256]{1,0:T(8,128)(2,1)S(1)} %get-tuple-element.96), channel_id=1, source_target_pairs={{0,12},{1,13},{2,14},{3,15},{4,8},{5,9},{6,10},{7,11},{8,4},{9,5},... | collective-permute-start | bytes 196616 | tf_op jit(solution)/shard_map/ppermute | solution.py:408
  52.6 1.2 %shard_map.70 = bf16[128,256]{1,0:T(8,128)(2,1)S(1)} custom-call(bf16[128,256]{1,0:T(8,128)(2,1)S(1)} %collective-permute-done.query_ref, bf16[2,128,128]{2,1,0:T(8,128)(2,1)S(1)} %get-tuple-element.86.refs_0_.refs_21_, bf16[2,256,128]{2,1,0:T(8,128)(2,1)S(1)} %get-tuple-element.87.refs_1_.refs_22_, ...), custom_call_target="tpu_custom_call" | custom-call | flops 268435456 | bytes 1048576 | tf_op jit(solution)/shard_map/pallas_call | solution.py:347
  53.8 2.6 %collective-permute-start.16 = (bf16[128,256]{1,0:T(8,128)(2,1)S(1)}, bf16[128,256]{1,0:T(8,128)(2,1)S(1)}, u32[]{:S(2)}, u32[]{:S(2)}) collective-permute-start(bf16[128,256]{1,0:T(8,128)(2,1)S(1)} %shard_map.70), channel_id=1, source_target_pairs={{0,14},{1,15},{2,12},{3,13},{4,10},{5,11},{6,8},{7,9},{8,6},{9,7},... | collective-permute-start | bytes 196616 | tf_op jit(solution)/shard_map/ppermute | solution.py:408
  56.5 0.8 %shard_map.71 = (bf16[128,256]{1,0:T(8,128)(2,1)S(1)}, bf16[128,256]{1,0:T(8,128)(2,1)S(1)}, bf16[128,256]{1,0:T(8,128)(2,1)S(1)}, bf16[128,256]{1,0:T(8,128)(2,1)S(1)}) custom-call(f32[3,256]{1,0:T(4,128)S(1)} %get-tuple-element.56.gain_ref, f32[2,384,128]{2,1,0:T(8,128)S(1)} %get-tuple-element.76.refs_0_.refs_6_, ...), custom_call_target="tpu_custom_call" | custom-call | flops 134217728 | bytes 1048576 | tf_op jit(solution)/shard_map/pallas_call | solution.py:347
  57.2 1.6 %collective-permute-start.17 = (bf16[128,256]{1,0:T(8,128)(2,1)S(1)}, bf16[128,256]{1,0:T(8,128)(2,1)S(1)}, u32[]{:S(2)}, u32[]{:S(2)}) collective-permute-start(bf16[128,256]{1,0:T(8,128)(2,1)S(1)} %get-tuple-element.92), channel_id=1, source_target_pairs={{0,2},{1,3},{2,0},{3,1},{4,6},{5,7},{6,4},{7,5},{8,10},{9,11},{10,... | collective-permute-start | bytes 196616 | tf_op jit(solution)/shard_map/ppermute | solution.py:408
  58.8 1.3 %collective-permute-start.22 = (bf16[128,256]{1,0:T(8,128)(2,1)S(1)}, bf16[128,256]{1,0:T(8,128)(2,1)S(1)}, u32[]{:S(2)}, u32[]{:S(2)}) collective-permute-start(bf16[128,256]{1,0:T(8,128)(2,1)S(1)} %get-tuple-element.98), channel_id=1, source_target_pairs={{0,10},{1,11},{2,8},{3,9},{4,14},{5,15},{6,12},{7,13},{8,2},{9,3},... | collective-permute-start | bytes 196616 | tf_op jit(solution)/shard_map/ppermute | solution.py:408
  60.1 1.4 %collective-permute-start.18 = (bf16[128,256]{1,0:T(8,128)(2,1)S(1)}, bf16[128,256]{1,0:T(8,128)(2,1)S(1)}, u32[]{:S(2)}, u32[]{:S(2)}) collective-permute-start(bf16[128,256]{1,0:T(8,128)(2,1)S(1)} %get-tuple-element.93), channel_id=1, source_target_pairs={{0,6},{1,7},{2,4},{3,5},{4,2},{5,3},{6,0},{7,1},{8,14},{9,15},{10,... | collective-permute-start | bytes 196616 | tf_op jit(solution)/shard_map/ppermute | solution.py:408
  61.5 1.8 %collective-permute-start.19 = (bf16[128,256]{1,0:T(8,128)(2,1)S(1)}, bf16[128,256]{1,0:T(8,128)(2,1)S(1)}, u32[]{:S(2)}, u32[]{:S(2)}) collective-permute-start(bf16[128,256]{1,0:T(8,128)(2,1)S(1)} %get-tuple-element.94), channel_id=1, source_target_pairs={{0,4},{1,5},{2,6},{3,7},{4,0},{5,1},{6,2},{7,3},{8,12},{9,13},{10,... | collective-permute-start | bytes 196616 | tf_op jit(solution)/shard_map/ppermute | solution.py:408
  63.2 2.4 %collective-permute-done.22.refs_3_ = bf16[128,256]{1,0:T(8,128)(2,1)S(1)} collective-permute-done((bf16[128,256]{1,0:T(8,128)(2,1)S(1)}, bf16[128,256]{1,0:T(8,128)(2,1)S(1)}, u32[]{:S(2)}, u32[]{:S(2)}) %collective-permute-start.22) | collective-permute-done | bytes 65568 | tf_op jit(solution)/shard_map/ppermute | solution.py:408
  66.4 0.7 %shard_map.73 = bf16[128,2048]{1,0:T(8,128)(2,1)} custom-call(bf16[128,256]{1,0:T(8,128)(2,1)S(1)} %collective-permute-done.16.refs_0_, bf16[128,256]{1,0:T(8,128)(2,1)S(1)} %collective-permute-done.17.refs_1_, bf16[128,256]{1,0:T(8,128)(2,1)S(1)} %collective-permute-done.18.refs_2_, ...), custom_call_target="tpu_custom_call", output_to_operand_aliasing={{}: (4, {})} | custom-call | tf_op jit(solution)/shard_map/pallas_call | solution.py:465
  (32 shorter events, 4.0 us)
Async XLA Ops:
  1.1 20.1 %collective-permute-start.1 = (bf16[392,256]{1,0:T(8,128)(2,1)S(1)}, bf16[392,256]{1,0:T(8,128)(2,1)S(1)}, u32[]{:S(2)}, u32[]{:S(2)}) collective-permute-start(bf16[392,256]{1,0:T(8,128)(2,1)S(1)} %get-tuple-element.54), channel_id=1, source_target_pairs={{0,4},{1,5},{2,6},{3,7},{4,0},{5,1},{6,2},{7,3},{8,12},{9,13},{10,... | collective-permute-start | bytes 602120 | tf_op jit(solution)/shard_map/ppermute | solution.py:408
  4.2 23.4 %collective-permute-start.2 = (bf16[392,256]{1,0:T(8,128)(2,1)S(1)}, bf16[392,256]{1,0:T(8,128)(2,1)S(1)}, u32[]{:S(2)}, u32[]{:S(2)}) collective-permute-start(bf16[392,256]{1,0:T(8,128)(2,1)S(1)} %get-tuple-element.55), channel_id=1, source_target_pairs={{0,8},{1,9},{2,10},{3,11},{4,12},{5,13},{6,14},{7,15},{8,0},{9,1},... | collective-permute-start | bytes 602120 | tf_op jit(solution)/shard_map/ppermute | solution.py:408
  8.3 12.4 %collective-permute-start.14 = (bf16[264,256]{1,0:T(8,128)(2,1)S(1)}, bf16[264,256]{1,0:T(8,128)(2,1)S(1)}, u32[]{:S(2)}, u32[]{:S(2)}) collective-permute-start(bf16[264,256]{1,0:T(8,128)(2,1)S(1)} %get-tuple-element.85), channel_id=1, source_target_pairs={{0,14},{1,15},{2,12},{3,13},{4,10},{5,11},{6,8},{7,9},{8,6},{9,7},... | collective-permute-start | bytes 405512 | tf_op jit(solution)/shard_map/ppermute | solution.py:408
  9.6 19.4 %collective-permute-start.3 = (bf16[392,256]{1,0:T(8,128)(2,1)S(1)}, bf16[392,256]{1,0:T(8,128)(2,1)S(1)}, u32[]{:S(2)}, u32[]{:S(2)}) collective-permute-start(bf16[392,256]{1,0:T(8,128)(2,1)S(1)} %get-tuple-element.53.refs_0_), channel_id=1, source_target_pairs={{0,1},{1,0},{2,3},{3,2},{4,5},{5,4},{6,7},{7,6},{8,9},{9,8},{10,11... | collective-permute-start | bytes 602120 | tf_op jit(solution)/shard_map/ppermute | solution.py:422
  9.6 19.4 %collective-permute-start.6 = (bf16[392,256]{1,0:T(8,128)(2,1)S(1)}, bf16[392,256]{1,0:T(8,128)(2,1)S(1)}, u32[]{:S(2)}, u32[]{:S(2)}) collective-permute-start(bf16[392,256]{1,0:T(8,128)(2,1)S(1)} %get-tuple-element.64), channel_id=1, source_target_pairs={{0,6},{1,7},{2,4},{3,5},{4,2},{5,3},{6,0},{7,1},{8,14},{9,15},{10,... | collective-permute-start | bytes 602120 | tf_op jit(solution)/shard_map/ppermute | solution.py:408
  20.7 8.7 %collective-permute-start.7 = (bf16[392,256]{1,0:T(8,128)(2,1)S(1)}, bf16[392,256]{1,0:T(8,128)(2,1)S(1)}, u32[]{:S(2)}, u32[]{:S(2)}) collective-permute-start(bf16[392,256]{1,0:T(8,128)(2,1)S(1)} %get-tuple-element.65), channel_id=1, source_target_pairs={{0,2},{1,3},{2,0},{3,1},{4,6},{5,7},{6,4},{7,5},{8,10},{9,11},{10,... | collective-permute-start | bytes 602120 | tf_op jit(solution)/shard_map/ppermute | solution.py:408
  21.3 19.2 %collective-permute-start.8 = (bf16[392,256]{1,0:T(8,128)(2,1)S(1)}, bf16[392,256]{1,0:T(8,128)(2,1)S(1)}, u32[]{:S(2)}, u32[]{:S(2)}) collective-permute-start(bf16[392,256]{1,0:T(8,128)(2,1)S(1)} %get-tuple-element.66), channel_id=1, source_target_pairs={{0,10},{1,11},{2,8},{3,9},{4,14},{5,15},{6,12},{7,13},{8,2},{9,3},... | collective-permute-start | bytes 602120 | tf_op jit(solution)/shard_map/ppermute | solution.py:408
  27.7 12.8 %collective-permute-start.12 = (bf16[392,256]{1,0:T(8,128)(2,1)S(1)}, bf16[392,256]{1,0:T(8,128)(2,1)S(1)}, u32[]{:S(2)}, u32[]{:S(2)}) collective-permute-start(bf16[392,256]{1,0:T(8,128)(2,1)S(1)} %get-tuple-element.75), channel_id=1, source_target_pairs={{0,12},{1,13},{2,14},{3,15},{4,8},{5,9},{6,10},{7,11},{8,4},{9,5},... | collective-permute-start | bytes 602120 | tf_op jit(solution)/shard_map/ppermute | solution.py:408
  28.9 12.0 %collective-permute-start.4 = (bf16[392,256]{1,0:T(8,128)(2,1)S(1)}, bf16[392,256]{1,0:T(8,128)(2,1)S(1)}, u32[]{:S(2)}, u32[]{:S(2)}) collective-permute-start(bf16[392,256]{1,0:T(8,128)(2,1)S(1)} %collective-permute-done.1.refs_1_), channel_id=1, source_target_pairs={{0,1},{1,0},{2,3},{3,2},{4,5},{5,4},{6,7},{7,6},{8,9},{9,8},{10,11... | collective-permute-start | bytes 602120 | tf_op jit(solution)/shard_map/ppermute | solution.py:422
  28.9 12.1 %collective-permute-start.5 = (bf16[392,256]{1,0:T(8,128)(2,1)S(1)}, bf16[392,256]{1,0:T(8,128)(2,1)S(1)}, u32[]{:S(2)}, u32[]{:S(2)}) collective-permute-start(bf16[392,256]{1,0:T(8,128)(2,1)S(1)} %collective-permute-done.2.refs_2_), channel_id=1, source_target_pairs={{0,1},{1,0},{2,3},{3,2},{4,5},{5,4},{6,7},{7,6},{8,9},{9,8},{10,11... | collective-permute-start | bytes 602120 | tf_op jit(solution)/shard_map/ppermute | solution.py:422
  29.4 13.9 %collective-permute-start.9 = (bf16[392,256]{1,0:T(8,128)(2,1)S(1)}, bf16[392,256]{1,0:T(8,128)(2,1)S(1)}, u32[]{:S(2)}, u32[]{:S(2)}) collective-permute-start(bf16[392,256]{1,0:T(8,128)(2,1)S(1)} %collective-permute-done.6.refs_7_), channel_id=1, source_target_pairs={{0,1},{1,0},{2,3},{3,2},{4,5},{5,4},{6,7},{7,6},{8,9},{9,8},{10,11... | collective-permute-start | bytes 602120 | tf_op jit(solution)/shard_map/ppermute | solution.py:422
  40.4 5.3 %collective-permute-start.10 = (bf16[392,256]{1,0:T(8,128)(2,1)S(1)}, bf16[392,256]{1,0:T(8,128)(2,1)S(1)}, u32[]{:S(2)}, u32[]{:S(2)}) collective-permute-start(bf16[392,256]{1,0:T(8,128)(2,1)S(1)} %collective-permute-done.7.refs_8_), channel_id=1, source_target_pairs={{0,1},{1,0},{2,3},{3,2},{4,5},{5,4},{6,7},{7,6},{8,9},{9,8},{10,11... | collective-permute-start | bytes 602120 | tf_op jit(solution)/shard_map/ppermute | solution.py:422
  40.4 5.3 %collective-permute-start.11 = (bf16[392,256]{1,0:T(8,128)(2,1)S(1)}, bf16[392,256]{1,0:T(8,128)(2,1)S(1)}, u32[]{:S(2)}, u32[]{:S(2)}) collective-permute-start(bf16[392,256]{1,0:T(8,128)(2,1)S(1)} %collective-permute-done.8.refs_9_), channel_id=1, source_target_pairs={{0,1},{1,0},{2,3},{3,2},{4,5},{5,4},{6,7},{7,6},{8,9},{9,8},{10,11... | collective-permute-start | bytes 602120 | tf_op jit(solution)/shard_map/ppermute | solution.py:422
  40.9 7.4 %collective-permute-start.13 = (bf16[392,256]{1,0:T(8,128)(2,1)S(1)}, bf16[392,256]{1,0:T(8,128)(2,1)S(1)}, u32[]{:S(2)}, u32[]{:S(2)}) collective-permute-start(bf16[392,256]{1,0:T(8,128)(2,1)S(1)} %collective-permute-done.12.refs_14_), channel_id=1, source_target_pairs={{0,1},{1,0},{2,3},{3,2},{4,5},{5,4},{6,7},{7,6},{8,9},{9,8},{10,11... | collective-permute-start | bytes 602120 | tf_op jit(solution)/shard_map/ppermute | solution.py:422
  41.0 9.0 %collective-permute-start.15 = (bf16[264,256]{1,0:T(8,128)(2,1)S(1)}, bf16[264,256]{1,0:T(8,128)(2,1)S(1)}, u32[]{:S(2)}, u32[]{:S(2)}) collective-permute-start(bf16[264,256]{1,0:T(8,128)(2,1)S(1)} %collective-permute-done.14.refs_21_), channel_id=1, source_target_pairs={{0,1},{1,0},{2,3},{3,2},{4,5},{5,4},{6,7},{7,6},{8,9},{9,8},{10,11... | collective-permute-start | bytes 405512 | tf_op jit(solution)/shard_map/ppermute | solution.py:422
  43.3 9.3 %collective-permute-start = (bf16[128,256]{1,0:T(8,128)(2,1)S(1)}, bf16[128,256]{1,0:T(8,128)(2,1)S(1)}, u32[]{:S(2)}, u32[]{:S(2)}) collective-permute-start(bf16[128,256]{1,0:T(8,128)(2,1)S(1)} %get-tuple-element.52), channel_id=1, source_target_pairs={{0,14},{1,15},{2,12},{3,13},{4,10},{5,11},{6,8},{7,9},{8,6},{9,7},... | collective-permute-start | bytes 196616 | tf_op jit(solution)/shard_map/ppermute | solution.py:408
  50.8 9.3 %collective-permute-start.20 = (bf16[128,256]{1,0:T(8,128)(2,1)S(1)}, bf16[128,256]{1,0:T(8,128)(2,1)S(1)}, u32[]{:S(2)}, u32[]{:S(2)}) collective-permute-start(bf16[128,256]{1,0:T(8,128)(2,1)S(1)} %get-tuple-element.96), channel_id=1, source_target_pairs={{0,12},{1,13},{2,14},{3,15},{4,8},{5,9},{6,10},{7,11},{8,4},{9,5},... | collective-permute-start | bytes 196616 | tf_op jit(solution)/shard_map/ppermute | solution.py:408
  52.1 9.3 %collective-permute-start.21 = (bf16[128,256]{1,0:T(8,128)(2,1)S(1)}, bf16[128,256]{1,0:T(8,128)(2,1)S(1)}, u32[]{:S(2)}, u32[]{:S(2)}) collective-permute-start(bf16[128,256]{1,0:T(8,128)(2,1)S(1)} %get-tuple-element.97), channel_id=1, source_target_pairs={{0,8},{1,9},{2,10},{3,11},{4,12},{5,13},{6,14},{7,15},{8,0},{9,1},... | collective-permute-start | bytes 196616 | tf_op jit(solution)/shard_map/ppermute | solution.py:408
  53.8 12.6 %collective-permute-start.16 = (bf16[128,256]{1,0:T(8,128)(2,1)S(1)}, bf16[128,256]{1,0:T(8,128)(2,1)S(1)}, u32[]{:S(2)}, u32[]{:S(2)}) collective-permute-start(bf16[128,256]{1,0:T(8,128)(2,1)S(1)} %shard_map.70), channel_id=1, source_target_pairs={{0,14},{1,15},{2,12},{3,13},{4,10},{5,11},{6,8},{7,9},{8,6},{9,7},... | collective-permute-start | bytes 196616 | tf_op jit(solution)/shard_map/ppermute | solution.py:408
  57.2 9.2 %collective-permute-start.17 = (bf16[128,256]{1,0:T(8,128)(2,1)S(1)}, bf16[128,256]{1,0:T(8,128)(2,1)S(1)}, u32[]{:S(2)}, u32[]{:S(2)}) collective-permute-start(bf16[128,256]{1,0:T(8,128)(2,1)S(1)} %get-tuple-element.92), channel_id=1, source_target_pairs={{0,2},{1,3},{2,0},{3,1},{4,6},{5,7},{6,4},{7,5},{8,10},{9,11},{10,... | collective-permute-start | bytes 196616 | tf_op jit(solution)/shard_map/ppermute | solution.py:408
  58.8 6.8 %collective-permute-start.22 = (bf16[128,256]{1,0:T(8,128)(2,1)S(1)}, bf16[128,256]{1,0:T(8,128)(2,1)S(1)}, u32[]{:S(2)}, u32[]{:S(2)}) collective-permute-start(bf16[128,256]{1,0:T(8,128)(2,1)S(1)} %get-tuple-element.98), channel_id=1, source_target_pairs={{0,10},{1,11},{2,8},{3,9},{4,14},{5,15},{6,12},{7,13},{8,2},{9,3},... | collective-permute-start | bytes 196616 | tf_op jit(solution)/shard_map/ppermute | solution.py:408
  60.1 6.3 %collective-permute-start.18 = (bf16[128,256]{1,0:T(8,128)(2,1)S(1)}, bf16[128,256]{1,0:T(8,128)(2,1)S(1)}, u32[]{:S(2)}, u32[]{:S(2)}) collective-permute-start(bf16[128,256]{1,0:T(8,128)(2,1)S(1)} %get-tuple-element.93), channel_id=1, source_target_pairs={{0,6},{1,7},{2,4},{3,5},{4,2},{5,3},{6,0},{7,1},{8,14},{9,15},{10,... | collective-permute-start | bytes 196616 | tf_op jit(solution)/shard_map/ppermute | solution.py:408
  61.5 5.0 %collective-permute-start.19 = (bf16[128,256]{1,0:T(8,128)(2,1)S(1)}, bf16[128,256]{1,0:T(8,128)(2,1)S(1)}, u32[]{:S(2)}, u32[]{:S(2)}) collective-permute-start(bf16[128,256]{1,0:T(8,128)(2,1)S(1)} %get-tuple-element.94), channel_id=1, source_target_pairs={{0,4},{1,5},{2,6},{3,7},{4,0},{5,1},{6,2},{7,3},{8,12},{9,13},{10,... | collective-permute-start | bytes 196616 | tf_op jit(solution)/shard_map/ppermute | solution.py:408
